TPU v7x, 768 devices: a whole 4x8x12 slice. The times are simulated.
768 devices in a mesh: replica: 8 (over x, core), fsdp: 24 (over y_lo, z), tensor: 4 (over y_hi).
Axes of the slice: x: 4, y: 8 (y_hi: 4, y_lo: 2; y = y_hi * 2 + y_lo), z: 12, core: 2. Of those that a mesh axis runs over, the one named last changes fastest.
Arguments:
- pseudo_grad: bfloat16 [8, 3072, 18432], P('replica', 'fsdp', 'tensor'), may hold values from -6 to 6
- compensation: float32 [8, 3072, 18432], P('replica', 'fsdp', 'tensor'), may hold values from -6 to 6
- params: float32 [3072, 18432], P(('fsdp', 'replica'), 'tensor'), may hold values from -6 to 6
- momentum: float32 [3072, 18432], P(('fsdp', 'replica'), 'tensor'), may hold values from -6 to 6
- probe: bfloat16 [1536, 18432], P('fsdp', 'tensor'), may hold values from -0.046875 to 0.046875
Outputs:
- new_params: float32 [3072, 18432], P(('fsdp', 'replica'), 'tensor')
- new_momentum: float32 [3072, 18432], P(('fsdp', 'replica'), 'tensor')
- probe_out: bfloat16 [1536, 3072], P('tensor', 'fsdp')
All inputs are finite; a program needn't handle non-finite values.
Results may differ from a plain program's by a relative error of at most 0.014.
Values may be sent and summed in bfloat16 or wider, within the bound.
No kernel may reach another device: no remote copies, remote signals or barrier semaphores. Data moves between devices by JAX's collectives and lax.ppermute only.
A program may use at most 64 MiB of HBM per device.

v0:
```python
import jax
import jax.numpy as jnp
from jax import lax
from jax.sharding import PartitionSpec as P

outer_rate = 0.7
nesterov = 0.9


def split_up(x, dim, size):
    shape = x.shape
    tiles = x.reshape(*shape[:dim], size, shape[dim] // size, *shape[dim + 1 :])
    return jnp.moveaxis(tiles, dim, 0)


def summed_on_arrival(x, axis, dim):
    tiles = split_up(x, dim, lax.axis_size(axis))
    arrived = lax.all_to_all(tiles, axis, split_axis=0, concat_axis=0, tiled=True)
    return arrived.astype(jnp.float32).sum(axis=0)


def sent_to_all(x, axis):
    copies = jnp.broadcast_to(x, (lax.axis_size(axis), *x.shape))
    return lax.all_to_all(copies, axis, split_axis=0, concat_axis=0, tiled=True)


def in_order(tiles, dim):
    shape = list(tiles.shape[1:])
    shape[dim] *= tiles.shape[0]
    return jnp.moveaxis(tiles, 0, dim).reshape(shape)


def gathered_copies(x, axis, dim):
    tiles = sent_to_all(x, axis)
    return in_order(tiles, dim)


def per_device(pseudo_grad, compensation, params, momentum, probe):
    outgoing = (pseudo_grad[0].astype(jnp.float32) + compensation[0]).astype(jnp.bfloat16)
    summed = summed_on_arrival(outgoing, "replica", 0)
    average = summed / lax.axis_size("replica")
    new_momentum = nesterov * momentum + average
    new_params = params - outer_rate * (average + nesterov * new_momentum)
    weights = new_params.astype(jnp.bfloat16)
    local_weights = gathered_copies(weights, "replica", 0)
    workers = lax.axis_size("replica")
    strided = probe.reshape(probe.shape[0] // workers, workers, probe.shape[1])
    picked = lax.dynamic_slice_in_dim(strided, lax.axis_index("replica"), 1, 1)
    source_rows = picked.reshape(probe.shape[0] // workers, probe.shape[1])
    partial_value = lax.dot_general(
        lax.all_gather(source_rows, "fsdp", axis=0, tiled=True),
        local_weights,
        (((1,), (1,)), ((), ())),
        preferred_element_type=jnp.float32,
    )
    chosen_part = summed_on_arrival(partial_value.astype(jnp.bfloat16), "tensor", 0).astype(
        jnp.bfloat16
    )
    joined = gathered_copies(chosen_part, "replica", 0)
    block_rows = chosen_part.shape[0]
    width = chosen_part.shape[1]
    probe_out = (
        joined.reshape(workers, block_rows, width)
        .transpose(1, 0, 2)
        .reshape(workers * block_rows, width)
    )
    return (new_params, new_momentum, probe_out)


def solution(mesh):
    in_specs = (
        P("replica", "fsdp", "tensor"),
        P("replica", "fsdp", "tensor"),
        P(("fsdp", "replica"), "tensor"),
        P(("fsdp", "replica"), "tensor"),
        P("fsdp", "tensor"),
    )
    out_specs = (
        P(("fsdp", "replica"), "tensor"),
        P(("fsdp", "replica"), "tensor"),
        P("tensor", "fsdp"),
    )
    return jax.shard_map(
        per_device, mesh=mesh, in_specs=in_specs, out_specs=out_specs, check_vma=False
    )
```

profile of v0, /device:TPU:1, one launch (start us, length us, event | category | flops | bytes accessed | tf_op | source)
XLA Modules:
  0.0 165.9 jit_solution(863678869579234715)
XLA Ops:
  7.2 0.0 copy-start
  7.2 3.2 %add_convert_fusion = bf16[1,128,4608]{2,1,0:T(8,128)(2,1)} fusion(f32[1,128,4608]{2,1,0:T(8,128)} %param.6, bf16[1,128,4608]{2,1,0:T(8,128)(2,1)} %param.5), kind=kLoop, calls=%fused_computation.1 | loop fusion | flops 1769472 | bytes 4718592 | tf_op jit(solution)/shard_map/convert_element_type | solution.py:39
  10.4 13.9 %all-to-all-start = ((bf16[8,16,4608]{2,1,0:T(8,128)(2,1)}), bf16[8,16,4608]{2,1,0:T(8,128)(2,1)S(1)}, u32[]{:S(2)}, u32[]{:S(2)}) async-start(bf16[8,16,4608]{2,1,0:T(8,128)(2,1)} %bitcast), calls=%async_computation | async-start | bytes 2359296 | tf_op jit(solution)/shard_map/all_to_all | solution.py:18
  24.4 0.0 copy-start.1
  24.4 0.0 copy-start.2
  24.4 0.0 all-gather.3.cloned.1.call-start
  24.4 0.0 copy-done
  24.4 0.2 constant_dynamic-slice_fusion
  24.6 0.6 copy.9
  25.2 0.0 all-gather.3.cloned.1.call-update
  25.3 15.5 %all-to-all-done = bf16[8,16,4608]{2,1,0:T(8,128)(2,1)S(1)} async-done(((bf16[8,16,4608]{2,1,0:T(8,128)(2,1)}), bf16[8,16,4608]{2,1,0:T(8,128)(2,1)S(1)}, u32[]{:S(2)}, u32[]{:S(2)}) %all-to-all-start) | async-done | bytes 1179680 | tf_op jit(solution)/shard_map/all_to_all | solution.py:18
  40.8 0.2 convert_reduce_fusion
  40.9 0.0 copy-done.1
  40.9 0.0 copy-done.2
  40.9 0.9 fusion.5
  41.8 0.1 broadcast_in_dim.6
  41.9 19.9 %all_to_all.20 = bf16[8,16,4608]{2,1,0:T(8,128)(2,1)S(1)} all-to-all(bf16[8,16,4608]{2,1,0:T(8,128)(2,1)S(1)} %broadcast_in_dim.6), channel_id=1, replica_groups=mesh['replica'=8,'fsdp'=24,'tensor'=4] {'replica'}, dimensions={0} | all-to-all | bytes 2359296 | tf_op jit(solution)/shard_map/all_to_all | solution.py:24
  61.8 54.6 %all-gather.3.cloned.1.call-done = bf16[192,1,4608]{2,0,1:T(8,128)(2,1)} async-done(((bf16[8,1,4608]{2,0,1:T(8,128)(2,1)}), bf16[192,1,4608]{2,0,1:T(8,128)(2,1)}) %all-gather.3.cloned.1.call-update) | async-done | bytes 1769488 | tf_op jit(solution)/shard_map/all_gather | solution.py:51
  116.4 2.1 %fusion.2 = bf16[192,128]{1,0:T(8,128)(2,1)S(1)} fusion(bf16[128,4608]{1,0:T(8,128)(2,1)S(1)} %bitcast.16, bf16[192,1,4608]{2,0,1:T(8,128)(2,1)} %all-gather.3.cloned.1.call-done), kind=kOutput, calls=%fused_computation.4 | convolution fusion | flops 226516992 | bytes 2998272 | tf_op jit(solution)/shard_map/dot_general | solution.py:50
  118.5 12.5 %all_to_all.21 = bf16[4,48,128]{2,1,0:T(8,128)(2,1)S(1)} all-to-all(bf16[4,48,128]{2,1,0:T(8,128)(2,1)S(1)} %bitcast.17), channel_id=1, replica_groups=mesh['replica'=8,'fsdp'=24,'tensor'=4] {'tensor'}, dimensions={0} | all-to-all | bytes 98304 | tf_op jit(solution)/shard_map/all_to_all | solution.py:18
  131.0 27.3 %all_to_all.22 = bf16[8,48,128]{2,1,0:T(8,128)(2,1)S(1)} all-to-all(bf16[8,48,128]{2,1,0:T(8,128)(2,1)S(1)} %broadcast_in_dim.7), channel_id=1, replica_groups=mesh['replica'=8,'fsdp'=24,'tensor'=4] {'replica'}, dimensions={0} | all-to-all | bytes 196608 | tf_op jit(solution)/shard_map/all_to_all | solution.py:24
  158.4 0.7 copy.12
  (2 shorter events, 0.0 us)
Async XLA Ops:
  7.2 17.3 %copy-start = (bf16[64,4608]{1,0:T(8,128)(2,1)S(1)}, bf16[64,4608]{1,0:T(8,128)(2,1)}, u32[]{:S(2)}) copy-start(bf16[64,4608]{1,0:T(8,128)(2,1)} %param.9) | copy-start | bytes 1769476
  10.4 30.3 %all-to-all-start = ((bf16[8,16,4608]{2,1,0:T(8,128)(2,1)}), bf16[8,16,4608]{2,1,0:T(8,128)(2,1)S(1)}, u32[]{:S(2)}, u32[]{:S(2)}) async-start(bf16[8,16,4608]{2,1,0:T(8,128)(2,1)} %bitcast), calls=%async_computation | async-start | bytes 2359296 | tf_op jit(solution)/shard_map/all_to_all | solution.py:18
  24.4 16.6 %copy-start.1 = (f32[16,4608]{1,0:T(8,128)S(1)}, f32[16,4608]{1,0:T(8,128)}, u32[]{:S(2)}) copy-start(f32[16,4608]{1,0:T(8,128)} %param.7) | copy-start | bytes 884740
  24.4 16.6 %copy-start.2 = (f32[16,4608]{1,0:T(8,128)S(1)}, f32[16,4608]{1,0:T(8,128)}, u32[]{:S(2)}) copy-start(f32[16,4608]{1,0:T(8,128)} %param.8) | copy-start | bytes 884740
  24.4 92.0 %all-gather.3.cloned.1.call-start = ((), (), s32[]{:S(2)}) async-start(), calls=%async_computation.4 | async-start | bytes 1843200 | tf_op jit(solution)/shard_map/all_gather | solution.py:51
Sparse Core Ops, SparseCore 0:
  28.1 88.2 all-gather.2
where the time goes:
time: 166 us
  waiting for transfers between devices  70.1 us (42%)
  blocking collectives  59.7 us (36%)
  between operations  14.1 us (8%)
  starting transfers between devices  14 us (8%)
  other arithmetic  4.3 us (3%)
  matrix products  2.09 us (1%)
    all_gather x1, waiting for transfers between devices, per_device(): lax.all_gather(source_rows, 'fsdp', axis=0, tiled=True)  54.6 us
    all_to_all x2, blocking collectives, sent_to_all(): return lax.all_to_all(copies, axis, split_axis=0, concat_axis=0, tiled=True)  47.2 us
    all_to_all x1, waiting for transfers between devices, summed_on_arrival(): lax.all_to_all(tiles, axis, split_axis=0, concat_axis=0, tiled=True)  15.5 us
    all_to_all x1, starting transfers between devices, summed_on_arrival(): lax.all_to_all(tiles, axis, split_axis=0, concat_axis=0, tiled=True)  13.9 us
    all_to_all x1, blocking collectives, summed_on_arrival(): lax.all_to_all(tiles, axis, split_axis=0, concat_axis=0, tiled=True)  12.5 us
  transfers between devices with their start and end apart: 2, of which 2 were waited for; matrix products, arithmetic and copies ran while one was open for 1% of the time, Pallas kernels for 0%

commit v1 on v0

v1 whole, which is shorter than its diff:
```python
import functools

import jax
import jax.numpy as jnp
from jax import lax
from jax.experimental import pallas as pl
from jax.experimental.pallas import tpu as pltpu
from jax.sharding import Mesh
from jax.sharding import PartitionSpec as P


outer_rate = 0.7
nesterov = 0.9
f32, bf16 = jnp.float32, jnp.bfloat16

X, CORE, YLO, ZQ, ZR, YHI = 4, 2, 2, 4, 3, 4
Z = ZQ * ZR
Z_ORDER = [0, 1, 2, 3, 4, 5, 6, 7]
Y_ORDER = [4, 3, 2, 1, 0, 7, 6, 5]
X_ORDER = [2, 3, 0, 1]
ROWS = 16
COLS = 1152


def exchange(tiles, axes, order):
    return lax.all_to_all(tiles, axes, split_axis=0, concat_axis=0, tiled=True, axis_index_groups=[order])


def shifted(x, axes, n, by):
    return lax.ppermute(x, axes, [(i, (i + by) % n) for i in range(n)])


def taken(tiles, i):
    return lax.dynamic_index_in_dim(tiles, i, 0, keepdims=False)


VMEM = pl.BlockSpec(memory_space=pltpu.VMEM)
ANY = pl.BlockSpec(memory_space=pltpu.HBM)
SMALL = pltpu.CompilerParams(vmem_limit_bytes=8 << 20)


def spread(probe_ref, copies_ref, kept_ref, sems):
    core, at = lax.axis_index("core"), pl.multiple_of(lax.axis_index("x") * COLS, 128)
    loads, stores = [], []
    for ylo in range(YLO):
        row = pl.multiple_of((core * YLO + ylo) * 16, 16)
        source = probe_ref.at[pl.ds(row, 16), pl.ds(at, COLS)]
        loads.append(pltpu.make_async_copy(source, kept_ref.at[ylo], sems.at[ylo]))
        loads[-1].start()
    for ylo in range(YLO):
        loads[ylo].wait()
        for zq in range(ZQ):
            n = Z_ORDER.index(ylo * ZQ + zq)
            stores.append(pltpu.make_async_copy(kept_ref.at[ylo], copies_ref.at[n], sems.at[YLO + n]))
            stores[-1].start()
    for store in stores:
        store.wait()


def added(other, grads_ref, carried_ref, sums_ref, grad_ref, carry_ref, sems):
    core = lax.axis_index("core")
    half = 1 - core if other else core
    copies = []
    for x in range(X):
        row = pl.multiple_of((x * CORE + half) * ROWS, 16)
        pair = (
            pltpu.make_async_copy(grads_ref.at[0, pl.ds(row, ROWS)], grad_ref.at[x], sems.at[0, x]),
            pltpu.make_async_copy(carried_ref.at[0, pl.ds(row, ROWS)], carry_ref.at[x], sems.at[1, x]),
        )
        for copy in pair:
            copy.start()
        copies.append(pair)
    for x in range(X):
        for copy in copies[x]:
            copy.wait()
        sums_ref[x * ROWS : (x + 1) * ROWS] = (grad_ref[x].astype(f32) + carry_ref[x]).astype(bf16)


def outgoing(other, grads, carried):
    return pl.pallas_call(
        functools.partial(added, other),
        out_shape=jax.ShapeDtypeStruct((X * ROWS, X * COLS), bf16),
        in_specs=[ANY, ANY],
        out_specs=VMEM,
        scratch_shapes=[
            pltpu.VMEM((X, ROWS, X * COLS), bf16),
            pltpu.VMEM((X, ROWS, X * COLS), f32),
            pltpu.SemaphoreType.DMA((2, X)),
        ],
        name="lent" if other else "kept",
        compiler_params=SMALL,
    )(pltpu.with_memory_space_constraint(grads, pltpu.HBM), pltpu.with_memory_space_constraint(carried, pltpu.HBM))


def product(below_ref, far_ref, above_ref, gathered_ref, chunks_ref, weights_ref):
    for ylo in range(YLO):
        for x in range(X):
            for core in range(CORE):
                at = (x * CORE + core) * ROWS
                weights_ref[ylo, at : at + ROWS] = gathered_ref[core * YLO + ylo, x * ROWS : (x + 1) * ROWS]
    for place, ref in enumerate((below_ref, far_ref, above_ref)):
        rows = ref[...].reshape(YLO * ZQ * 16, COLS)
        for ylo in range(YLO):
            found = lax.dot_general(
                rows, weights_ref[ylo], (((1,), (1,)), ((), ())), preferred_element_type=f32
            ).astype(bf16)
            for block in range(YLO * ZQ):
                t, low = block // 2, block % 2
                at = (low * ZR + place) * 16
                row = Z_ORDER.index(block) * 16
                chunks_ref[Y_ORDER.index(t * YLO + ylo), at : at + 16] = found[row : row + 16]


def part_sums(parts_ref, average_ref, sent_ref):
    for ylo in range(YLO):
        total = sum(parts_ref[Y_ORDER.index(t * YLO + ylo)].astype(f32) for t in range(YHI)).astype(bf16)
        for x in range(X):
            sent_ref[x, ylo * 96 : (ylo + 1) * 96] = total
    for x in range(X):
        for k in range(9):
            at = YLO * 96 + k * ROWS
            sent_ref[X_ORDER.index(x), at : at + ROWS] = average_ref[x * ROWS : (x + 1) * ROWS, k * 128 : (k + 1) * 128]


def updates(joined_ref, params_ref, momentum_ref, half_ref, new_params_ref, new_momentum_ref):
    total = joined_ref[0, 0 : YLO * 96].astype(f32)
    for x in range(1, X):
        total = total + joined_ref[x, 0 : YLO * 96].astype(f32)
    half_ref[...] = total.astype(bf16)
    for x in range(X):
        for k in range(9):
            at, col = YLO * 96 + k * ROWS, x * COLS + k * 128
            average = joined_ref[X_ORDER.index(x), at : at + ROWS].astype(f32)
            moved = nesterov * momentum_ref[:, col : col + 128] + average
            new_momentum_ref[:, col : col + 128] = moved
            new_params_ref[:, col : col + 128] = params_ref[:, col : col + 128] - outer_rate * (
                average + nesterov * moved
            )


def placing(whole_ref, out_ref):
    for place in range(ZR):
        zr = lax.rem(lax.axis_index("zr") + (place + ZR - 1), ZR)
        for core in range(CORE):
            for ylo in range(YLO):
                for low in range(2):
                    row = (low * ZR + zr) * 64 + (core * YLO + ylo) * 16
                    at = ylo * 96 + (low * ZR + place) * 16
                    out_ref[pl.ds(pl.multiple_of(row, 16), 16)] = whole_ref[core, at : at + 16]


def per_device(pseudo_grad, compensation, params, momentum, probe):
    x = lax.axis_index("x")

    copies = pl.pallas_call(
        spread,
        out_shape=jax.ShapeDtypeStruct((YLO * ZQ, 16, COLS), bf16),
        in_specs=[ANY],
        out_specs=ANY,
        scratch_shapes=[pltpu.VMEM((YLO, 16, COLS), bf16), pltpu.SemaphoreType.DMA((YLO + YLO * ZQ,))],
        name="spread",
        compiler_params=SMALL,
    )(pltpu.with_memory_space_constraint(probe, pltpu.HBM))
    far = exchange(copies, ("ylo", "zq"), Z_ORDER)
    below = shifted(far, ("zq", "zr"), Z, 1)
    above = shifted(far, ("zq", "zr"), Z, -1)

    partners = shifted(outgoing(True, pseudo_grad, compensation), "core", CORE, 1)
    kept = outgoing(False, pseudo_grad, compensation)
    pair = (partners.astype(f32) + kept).astype(bf16)
    decayed = (params - (outer_rate * nesterov * nesterov) * momentum).astype(bf16)
    both = jnp.concatenate([pair, decayed], axis=0)

    def share(i):
        return lax.dynamic_slice_in_dim(both, lax.rem(x + i, X) * COLS, COLS, axis=1)

    arrived = [share(0)]
    for i in range(1, X):
        arrived.append(shifted(share(i), "x", X, i))
    average = sum(a[: X * ROWS].astype(f32) for a in arrived) / (X * CORE)
    places = jnp.stack([a[X * ROWS :] for a in arrived])
    base = jnp.concatenate([taken(places, lax.rem(x - i + X, X)) for i in range(X)]).astype(f32)
    weights = (base - (outer_rate * (1 + nesterov)) * average).astype(bf16)

    two = lax.all_gather(weights, "ylo", axis=0)
    local_weights = lax.all_gather(two, "core", axis=0)
    chunks = pl.pallas_call(
        product,
        out_shape=jax.ShapeDtypeStruct((YHI * YLO, 96, 128), bf16),
        in_specs=[VMEM] * 4,
        out_specs=VMEM,
        scratch_shapes=[pltpu.VMEM((YLO, 128, COLS), bf16)],
        name="product",
        compiler_params=SMALL,
    )(below, far, above, local_weights.reshape(CORE * YLO, X * ROWS, COLS))
    parts = exchange(chunks, ("yhi", "ylo"), Y_ORDER)
    sent = pl.pallas_call(
        part_sums,
        out_shape=jax.ShapeDtypeStruct((X, YLO * 96 + 9 * ROWS, 128), bf16),
        in_specs=[VMEM] * 2,
        out_specs=VMEM,
        name="part_sums",
        compiler_params=SMALL,
    )(parts, average.astype(bf16))
    joined = exchange(sent, "x", X_ORDER)
    half, new_params, new_momentum = pl.pallas_call(
        updates,
        out_shape=(
            jax.ShapeDtypeStruct((YLO * 96, 128), bf16),
            jax.ShapeDtypeStruct(params.shape, f32),
            jax.ShapeDtypeStruct(momentum.shape, f32),
        ),
        in_specs=[VMEM] * 3,
        out_specs=(VMEM,) * 3,
        name="updates",
        compiler_params=SMALL,
    )(joined, params, momentum)
    whole = lax.all_gather(half, "core", axis=0)
    probe_out = pl.pallas_call(
        placing,
        out_shape=jax.ShapeDtypeStruct((384, 128), bf16),
        in_specs=[VMEM],
        out_specs=VMEM,
        name="placing",
        compiler_params=SMALL,
    )(whole)
    return new_params, new_momentum, probe_out


def solution(mesh):
    fine = Mesh(
        mesh.devices.reshape(X, CORE, YLO, ZQ, ZR, YHI), ("x", "core", "ylo", "zq", "zr", "yhi")
    )
    whole, rows = ("x", "core"), ("ylo", "zq", "zr")
    shard = P((*rows, *whole), "yhi")
    in_specs = (P(whole, rows, "yhi"), P(whole, rows, "yhi"), shard, shard, P(rows, "yhi"))
    out_specs = (shard, shard, P("yhi", rows))

    return jax.shard_map(per_device, mesh=fine, in_specs=in_specs, out_specs=out_specs, check_vma=False)
```

time: 166 us -> 81.1 us (0.49)
  waiting for transfers between devices: 70.1 us -> 0.08 us
  blocking collectives: 59.7 us -> 33.4 us
  starting transfers between devices: 14 us -> 38.6 us
  between operations: 14.1 us -> 0.9 us
  Pallas kernels: 0 us -> 7.05 us
  other arithmetic: 4.3 us -> 0.41 us
  matrix products: 2.09 us -> 0 us
    all_gather x1 -> x0, waiting for transfers between devices: 54.6 us -> none  [per_device(): lax.all_gather(source_rows, 'fsdp', axis=0, tiled=True)]
    all_to_all x3 -> x2, blocking collectives: 59.7 us -> 20.3 us  [exchange(): lax.all_to_all(tiles, axes, split_axis=0, concat_axis=0, tiled=True, axis...]
    ppermute x0 -> x6, starting transfers between devices: none -> 32.3 us  [shifted(): return lax.ppermute(x, axes, [(i, (i + by) % n) for i in range(n)])]
    all_to_all x1, waiting for transfers between devices: 15.5 us -> 0.06 us  [exchange(): lax.all_to_all(tiles, axes, split_axis=0, concat_axis=0, tiled=True, axis...]
    all_gather x0 -> x3, blocking collectives: none -> 13.1 us  [the longest x1 4.95 us: per_device(): two = lax.all_gather(weights, 'ylo', axis=0)]
    all_to_all x1, starting transfers between devices: 13.9 us -> 6.27 us  [exchange(): lax.all_to_all(tiles, axes, split_axis=0, concat_axis=0, tiled=True, axis...]
    pallas_call x0 -> x7, Pallas kernels: none -> 7.05 us  [the longest x2 3.2 us: outgoing(): pl.pallas_call(functools.partial(added, other), out_shape=jax.ShapeDtypeS...]
    convert_element_type x2 -> x3, other arithmetic: 4.13 us -> 0.3 us  [the longest x1 0.14 us: per_device(): pair = (partners.astype(f32) + kept).astype(bf16)]
  transfers between devices with their start and end apart: 2 -> 7, of which waited for: 2 -> 1; matrix products, arithmetic and copies ran while one was open for 1% -> 1% of each run, Pallas kernels for 0% -> 4%
where the time goes in v1:
time: 81.1 us; the launch traced here: 80.5 us
  starting transfers between devices  38.6 us (48%)
  blocking collectives  33.4 us (41%)
  Pallas kernels  7.05 us (9%)
  between operations  0.9 us (1%)
    ppermute x6, starting transfers between devices, shifted(): return lax.ppermute(x, axes, [(i, (i + by) % n) for i in range(n)])  32.3 us
    all_to_all x2, blocking collectives, exchange(): lax.all_to_all(tiles, axes, split_axis=0, concat_axis=0, tiled=True, axis...  20.3 us
    all_to_all x1, starting transfers between devices, exchange(): lax.all_to_all(tiles, axes, split_axis=0, concat_axis=0, tiled=True, axis...  6.27 us
    all_gather x1, blocking collectives, per_device(): two = lax.all_gather(weights, 'ylo', axis=0)  4.95 us
    all_gather x1, blocking collectives, per_device(): local_weights = lax.all_gather(two, 'core', axis=0)  4.32 us
    all_gather x1, blocking collectives, per_device(): whole = lax.all_gather(half, 'core', axis=0)  3.84 us
    pallas_call x2, Pallas kernels, outgoing(): pl.pallas_call(functools.partial(added, other), out_shape=jax.ShapeDtypeS...  3.2 us
  transfers between devices with their start and end apart: 7, of which 1 were waited for; matrix products, arithmetic and copies ran while one was open for 1% of the time, Pallas kernels for 4%

profile of v1, /device:TPU:1, one launch (start us, length us, event | category | flops | bytes accessed | tf_op | source)
XLA Modules:
  0.0 80.5 jit_solution(4986917359122675690)
XLA Ops:
  0.6 1.6 %lent.1 = bf16[64,4608]{1,0:T(8,128)(2,1)S(1)} custom-call(bf16[1,128,4608]{2,1,0:T(8,128)(2,1)} %grads_ref.3, f32[1,128,4608]{2,1,0:T(8,128)} %carried_ref.3), custom_call_target="tpu_custom_call" | custom-call | tf_op jit(solution)/shard_map/lent/pallas_call | solution.py:80
  2.2 12.4 %collective-permute-start.2 = (bf16[64,4608]{1,0:T(8,128)(2,1)S(1)}, bf16[64,4608]{1,0:T(8,128)(2,1)S(1)}, u32[]{:S(2)}, u32[]{:S(2)}) collective-permute-start(bf16[64,4608]{1,0:T(8,128)(2,1)S(1)} %lent.1), channel_id=1, source_target_pairs={{0,96},{96,0},{1,97},{97,1},{2,98},{98,2},{3,99},{99,3},{4,100},{1... | collective-permute-start | bytes 1769480 | tf_op jit(solution)/shard_map/ppermute | solution.py:30
  14.6 1.6 %spread.1 = bf16[8,16,1152]{2,1,0:T(8,128)(2,1)} custom-call(bf16[64,4608]{1,0:T(8,128)(2,1)} %probe_ref.1), custom_call_target="tpu_custom_call" | custom-call | tf_op jit(solution)/shard_map/spread/pallas_call | solution.py:155
  16.2 6.3 %all-to-all-start = ((bf16[8,16,1152]{2,1,0:T(8,128)(2,1)}), bf16[8,16,1152]{2,1,0:T(8,128)(2,1)S(1)}, u32[]{:S(2)}, u32[]{:S(2)}) async-start(bf16[8,16,1152]{2,1,0:T(8,128)(2,1)} %spread.1), calls=%async_computation | async-start | bytes 589824 | tf_op jit(solution)/shard_map/all_to_all | solution.py:26
  22.5 0.0 copy-start
  22.5 0.0 copy-start.1
  22.5 1.6 %kept.1 = bf16[64,4608]{1,0:T(8,128)(2,1)S(1)} custom-call(bf16[1,128,4608]{2,1,0:T(8,128)(2,1)} %grads_ref.3, f32[1,128,4608]{2,1,0:T(8,128)} %carried_ref.3), custom_call_target="tpu_custom_call" | custom-call | tf_op jit(solution)/shard_map/kept/pallas_call | solution.py:80
  24.2 0.0 copy-done
  24.2 0.0 copy-done.1
  24.2 0.0 collective-permute-done.2
  24.2 0.1 add_convert_fusion
  24.4 0.1 fusion.1
  24.5 4.4 %collective-permute-start.5 = (bf16[80,1152]{1,0:T(8,128)(2,1)S(1)}, bf16[80,1152]{1,0:T(8,128)(2,1)S(1)}, u32[]{:S(2)}, u32[]{:S(2)}) collective-permute-start(bf16[80,1152]{1,0:T(8,128)(2,1)S(1)} %get-tuple-element.14), channel_id=1, source_target_pairs={{0,576},{192,0},{384,192},{576,384},{1,577},{193,1},{385,193},{577... | collective-permute-start | bytes 552968 | tf_op jit(solution)/shard_map/ppermute | solution.py:30
  28.9 2.4 %collective-permute-start.4 = (bf16[80,1152]{1,0:T(8,128)(2,1)S(1)}, bf16[80,1152]{1,0:T(8,128)(2,1)S(1)}, u32[]{:S(2)}, u32[]{:S(2)}) collective-permute-start(bf16[80,1152]{1,0:T(8,128)(2,1)S(1)} %get-tuple-element.13), channel_id=1, source_target_pairs={{0,384},{192,576},{384,0},{576,192},{1,385},{193,577},{385,1},{577... | collective-permute-start | bytes 552968 | tf_op jit(solution)/shard_map/ppermute | solution.py:30
  31.3 2.5 %collective-permute-start.3 = (bf16[80,1152]{1,0:T(8,128)(2,1)S(1)}, bf16[80,1152]{1,0:T(8,128)(2,1)S(1)}, u32[]{:S(2)}, u32[]{:S(2)}) collective-permute-start(bf16[80,1152]{1,0:T(8,128)(2,1)S(1)} %get-tuple-element.12), channel_id=1, source_target_pairs={{0,192},{192,384},{384,576},{576,0},{1,193},{193,385},{385,577},{5... | collective-permute-start | bytes 552968 | tf_op jit(solution)/shard_map/ppermute | solution.py:30
  33.8 0.1 all-to-all-done.far_ref
  33.9 8.7 %collective-permute-start = (bf16[8,16,1152]{2,1,0:T(8,128)(2,1)S(1)}, bf16[8,16,1152]{2,1,0:T(8,128)(2,1)S(1)}, u32[]{:S(2)}, u32[]{:S(2)}) collective-permute-start(bf16[8,16,1152]{2,1,0:T(8,128)(2,1)S(1)} %all-to-all-done.far_ref), channel_id=1, source_target_pairs={{0,4},{4,8},{8,12},{12,16},{16,20},{20,24},{24,28},{28,32},{32,36}... | collective-permute-start | bytes 884744 | tf_op jit(solution)/shard_map/ppermute | solution.py:30
  42.6 1.9 %collective-permute-start.1 = (bf16[8,16,1152]{2,1,0:T(8,128)(2,1)S(1)}, bf16[8,16,1152]{2,1,0:T(8,128)(2,1)S(1)}, u32[]{:S(2)}, u32[]{:S(2)}) collective-permute-start(bf16[8,16,1152]{2,1,0:T(8,128)(2,1)S(1)} %all-to-all-done.far_ref), channel_id=1, source_target_pairs={{0,44},{4,0},{8,4},{12,8},{16,12},{20,16},{24,20},{28,24},{32,28},... | collective-permute-start | bytes 884744 | tf_op jit(solution)/shard_map/ppermute | solution.py:30
  44.5 0.0 collective-permute-done.5
  44.5 0.0 collective-permute-done.4
  44.5 0.0 collective-permute-done.3
  44.6 0.1 multiply_convert_fusion
  44.8 5.0 %all-gather = bf16[128,1152]{1,0:T(8,128)(2,1)S(1)} all-gather(bf16[64,1152]{1,0:T(8,128)(2,1)S(1)} %get-tuple-element.10), channel_id=2, replica_groups=mesh['x'=4,'core'=2,'ylo'=2,'zq'=4,'zr'=3,'yhi'=4] {'ylo'}, dimensions={0}, use_global_device_ids=true | all-gather | bytes 442368 | tf_op jit(solution)/shard_map/all_gather | solution.py:185
  49.7 4.3 %all-gather.1.gathered_ref = bf16[4,64,1152]{2,1,0:T(8,128)(2,1)S(1)} all-gather(bf16[2,64,1152]{2,1,0:T(8,128)(2,1)S(1)} %bitcast.19), channel_id=3, replica_groups=mesh['x'=4,'core'=2,'ylo'=2,'zq'=4,'zr'=3,'yhi'=4] {'core'}, dimensions={0}, use_global_device_ids=true | all-gather | bytes 884736 | tf_op jit(solution)/shard_map/all_gather | solution.py:186
  54.0 0.0 collective-permute-done.below_ref
  54.0 0.0 collective-permute-done.1.above_ref
  54.1 0.7 product.1
  54.8 11.7 %all_to_all.15.parts_ref = bf16[8,96,128]{2,1,0:T(8,128)(2,1)S(1)} all-to-all(bf16[8,96,128]{2,1,0:T(8,128)(2,1)S(1)} %product.1), channel_id=1, replica_groups={{2,49,1,48,0,51,3,50},{6,53,5,52,4,55,7,54},{10,57,9,56,8,59,11,58},{14..., dimensions={0} | all-to-all | bytes 393216 | tf_op jit(solution)/shard_map/all_to_all | solution.py:26
  66.5 8.7 %all_to_all.16.joined_ref = bf16[4,336,128]{2,1,0:T(8,128)(2,1)S(1)} all-to-all(bf16[4,336,128]{2,1,0:T(8,128)(2,1)S(1)} %part_sums.1), channel_id=1, replica_groups={{384,576,0,192},{385,577,1,193},{386,578,2,194},{387,579,3,195},{388,58..., dimensions={0} | all-to-all | bytes 688128 | tf_op jit(solution)/shard_map/all_to_all | solution.py:26
  75.1 0.9 %updates.1 = (bf16[192,128]{1,0:T(8,128)(2,1)S(1)}, f32[16,4608]{1,0:T(8,128)}, f32[16,4608]{1,0:T(8,128)}) custom-call(bf16[4,336,128]{2,1,0:T(8,128)(2,1)S(1)} %all_to_all.16.joined_ref, f32[16,4608]{1,0:T(8,128)S(1)} %copy-done, f32[16,4608]{1,0:T(8,128)S(1)} %copy-done.1), custom_call_target="tpu_custom_call" | custom-call | tf_op jit(solution)/shard_map/updates/pallas_call | solution.py:206
  76.0 3.8 %all-gather.2 = bf16[384,128]{1,0:T(8,128)(2,1)S(1)} all-gather(bf16[192,128]{1,0:T(8,128)(2,1)S(1)} %get-tuple-element.8), channel_id=4, replica_groups=mesh['x'=4,'core'=2,'ylo'=2,'zq'=4,'zr'=3,'yhi'=4] {'core'}, dimensions={0}, use_global_device_ids=true | all-gather | bytes 147456 | tf_op jit(solution)/shard_map/all_gather | solution.py:218
  79.9 0.7 placing.1
  (8 shorter events, 0.2 us)
Async XLA Ops:
  2.2 22.0 %collective-permute-start.2 = (bf16[64,4608]{1,0:T(8,128)(2,1)S(1)}, bf16[64,4608]{1,0:T(8,128)(2,1)S(1)}, u32[]{:S(2)}, u32[]{:S(2)}) collective-permute-start(bf16[64,4608]{1,0:T(8,128)(2,1)S(1)} %lent.1), channel_id=1, source_target_pairs={{0,96},{96,0},{1,97},{97,1},{2,98},{98,2},{3,99},{99,3},{4,100},{1... | collective-permute-start | bytes 1769480 | tf_op jit(solution)/shard_map/ppermute | solution.py:30
  16.2 17.7 %all-to-all-start = ((bf16[8,16,1152]{2,1,0:T(8,128)(2,1)}), bf16[8,16,1152]{2,1,0:T(8,128)(2,1)S(1)}, u32[]{:S(2)}, u32[]{:S(2)}) async-start(bf16[8,16,1152]{2,1,0:T(8,128)(2,1)} %spread.1), calls=%async_computation | async-start | bytes 589824 | tf_op jit(solution)/shard_map/all_to_all | solution.py:26
  22.5 1.7 %copy-start = (f32[16,4608]{1,0:T(8,128)S(1)}, f32[16,4608]{1,0:T(8,128)}, u32[]{:S(2)}) copy-start(f32[16,4608]{1,0:T(8,128)} %params_ref.1) | copy-start | bytes 884740
  22.5 1.7 %copy-start.1 = (f32[16,4608]{1,0:T(8,128)S(1)}, f32[16,4608]{1,0:T(8,128)}, u32[]{:S(2)}) copy-start(f32[16,4608]{1,0:T(8,128)} %momentum_ref.1) | copy-start | bytes 884740
  24.5 20.0 %collective-permute-start.5 = (bf16[80,1152]{1,0:T(8,128)(2,1)S(1)}, bf16[80,1152]{1,0:T(8,128)(2,1)S(1)}, u32[]{:S(2)}, u32[]{:S(2)}) collective-permute-start(bf16[80,1152]{1,0:T(8,128)(2,1)S(1)} %get-tuple-element.14), channel_id=1, source_target_pairs={{0,576},{192,0},{384,192},{576,384},{1,577},{193,1},{385,193},{577... | collective-permute-start | bytes 552968 | tf_op jit(solution)/shard_map/ppermute | solution.py:30
  28.9 15.7 %collective-permute-start.4 = (bf16[80,1152]{1,0:T(8,128)(2,1)S(1)}, bf16[80,1152]{1,0:T(8,128)(2,1)S(1)}, u32[]{:S(2)}, u32[]{:S(2)}) collective-permute-start(bf16[80,1152]{1,0:T(8,128)(2,1)S(1)} %get-tuple-element.13), channel_id=1, source_target_pairs={{0,384},{192,576},{384,0},{576,192},{1,385},{193,577},{385,1},{577... | collective-permute-start | bytes 552968 | tf_op jit(solution)/shard_map/ppermute | solution.py:30
  31.3 13.3 %collective-permute-start.3 = (bf16[80,1152]{1,0:T(8,128)(2,1)S(1)}, bf16[80,1152]{1,0:T(8,128)(2,1)S(1)}, u32[]{:S(2)}, u32[]{:S(2)}) collective-permute-start(bf16[80,1152]{1,0:T(8,128)(2,1)S(1)} %get-tuple-element.12), channel_id=1, source_target_pairs={{0,192},{192,384},{384,576},{576,0},{1,193},{193,385},{385,577},{5... | collective-permute-start | bytes 552968 | tf_op jit(solution)/shard_map/ppermute | solution.py:30
  33.9 20.2 %collective-permute-start = (bf16[8,16,1152]{2,1,0:T(8,128)(2,1)S(1)}, bf16[8,16,1152]{2,1,0:T(8,128)(2,1)S(1)}, u32[]{:S(2)}, u32[]{:S(2)}) collective-permute-start(bf16[8,16,1152]{2,1,0:T(8,128)(2,1)S(1)} %all-to-all-done.far_ref), channel_id=1, source_target_pairs={{0,4},{4,8},{8,12},{12,16},{16,20},{20,24},{24,28},{28,32},{32,36}... | collective-permute-start | bytes 884744 | tf_op jit(solution)/shard_map/ppermute | solution.py:30
  42.6 11.5 %collective-permute-start.1 = (bf16[8,16,1152]{2,1,0:T(8,128)(2,1)S(1)}, bf16[8,16,1152]{2,1,0:T(8,128)(2,1)S(1)}, u32[]{:S(2)}, u32[]{:S(2)}) collective-permute-start(bf16[8,16,1152]{2,1,0:T(8,128)(2,1)S(1)} %all-to-all-done.far_ref), channel_id=1, source_target_pairs={{0,44},{4,0},{8,4},{12,8},{16,12},{20,16},{24,20},{28,24},{32,28},... | collective-permute-start | bytes 884744 | tf_op jit(solution)/shard_map/ppermute | solution.py:30

commit v2 on v1

v2 whole, which is shorter than its diff:
```python
import jax
import jax.numpy as jnp
from jax import lax
from jax.experimental import pallas as pl
from jax.experimental.pallas import tpu as pltpu
from jax.sharding import Mesh
from jax.sharding import PartitionSpec as P


outer_rate = 0.7
nesterov = 0.9
f32, bf16 = jnp.float32, jnp.bfloat16

X, CORE, YLO, ZQ, ZR, YHI = 4, 2, 2, 4, 3, 4
Z = ZQ * ZR
Y_ORDER = [4, 3, 2, 1, 0, 7, 6, 5]
X_ORDER = [2, 0, 1, 3]
ROWS = 16
COLS = 1152


def exchange(tiles, axes, orders):
    return lax.all_to_all(tiles, axes, split_axis=0, concat_axis=0, tiled=True, axis_index_groups=orders)


LEADS = (3, 3, 2)
FAR_ORDERS = [
    [(ylo * ZQ + (lead + n) % ZQ) * ZR + zr for ylo in range(YLO) for n in range(ZQ)] for zr, lead in enumerate(LEADS)
]


def far_place(ylo, zq, zr):
    lead = jnp.where(zr == 0, LEADS[0], jnp.where(zr == 1, LEADS[1], LEADS[2]))
    return ylo * ZQ + lax.rem(zq + ZQ - lead, ZQ)


def swapped(x, axes, pairs):
    return lax.ppermute(x, axes, [*pairs, *((j, i) for i, j in pairs)])


def taken(tiles, i):
    return lax.dynamic_index_in_dim(tiles, i, 0, keepdims=False)


VMEM = pl.BlockSpec(memory_space=pltpu.VMEM)
ANY = pl.BlockSpec(memory_space=pltpu.HBM)
SMALL = pltpu.CompilerParams(vmem_limit_bytes=8 << 20)


def started(other, grads_ref, carried_ref, grad_ref, carry_ref, sems):
    core = lax.axis_index("core")
    half = 1 - core if other else core
    copies = []
    for x in range(X):
        row = pl.multiple_of((x * CORE + half) * ROWS, 16)
        pair = (
            pltpu.make_async_copy(grads_ref.at[0, pl.ds(row, ROWS)], grad_ref.at[x], sems.at[0, x]),
            pltpu.make_async_copy(carried_ref.at[0, pl.ds(row, ROWS)], carry_ref.at[x], sems.at[1, x]),
        )
        for copy in pair:
            copy.start()
        copies.append(pair)
    return copies


def added(copies, sums_ref, grad_ref, carry_ref):
    for x in range(X):
        for copy in copies[x]:
            copy.wait()
        sums_ref[x * ROWS : (x + 1) * ROWS] = (grad_ref[x].astype(f32) + carry_ref[x]).astype(bf16)


def opening(probe_ref, grads_ref, carried_ref, copies_ref, lent_ref, kept_ref, grad_ref, carry_ref, sems, sums_sems):
    core, at = lax.axis_index("core"), pl.multiple_of(lax.axis_index("x") * COLS, 128)
    loads, stores = [], []
    for ylo in range(YLO):
        row = pl.multiple_of((core * YLO + ylo) * 16, 16)
        source = probe_ref.at[pl.ds(row, 16), pl.ds(at, COLS)]
        loads.append(pltpu.make_async_copy(source, kept_ref.at[ylo], sems.at[ylo]))
        loads[-1].start()
    copies = started(True, grads_ref, carried_ref, grad_ref, carry_ref, sums_sems)
    for ylo in range(YLO):
        loads[ylo].wait()
        for zq in range(ZQ):
            to = far_place(ylo, zq, lax.axis_index("zr"))
            stores.append(
                pltpu.make_async_copy(kept_ref.at[ylo], copies_ref.at[to], sems.at[YLO + ylo * ZQ + zq])
            )
            stores[-1].start()
    added(copies, lent_ref, grad_ref, carry_ref)
    for store in stores:
        store.wait()


def own_rows(grads_ref, carried_ref, sums_ref, grad_ref, carry_ref, sems):
    added(started(False, grads_ref, carried_ref, grad_ref, carry_ref, sems), sums_ref, grad_ref, carry_ref)


SUMS = jax.ShapeDtypeStruct((X * ROWS, X * COLS), bf16)
SUMS_SCRATCH = [
    pltpu.VMEM((X, ROWS, X * COLS), bf16),
    pltpu.VMEM((X, ROWS, X * COLS), f32),
]


def neighbour_zr(core):
    zr = lax.axis_index("zr")
    odd = lax.rem(lax.axis_index("zq") * ZR + zr + core, 2)
    return lax.rem(zr + 1 + odd, ZR)


def product(near_ref, far_ref, gathered_ref, chunks_ref, weights_ref, rows_ref):
    for ylo in range(YLO):
        for x in range(X):
            for core in range(CORE):
                at = (x * CORE + core) * ROWS
                weights_ref[ylo, at : at + ROWS] = gathered_ref[core * YLO + ylo, x * ROWS : (x + 1) * ROWS]
    near_zr = neighbour_zr(lax.axis_index("core"))
    for place in range(3):
        for block in range(YLO * ZQ):
            row = (place * YLO * ZQ + block) * 16
            if place < 2:
                rows_ref[row : row + 16] = near_ref[place, far_place(block // ZQ, block % ZQ, near_zr)]
            else:
                rows_ref[row : row + 16] = far_ref[far_place(block // ZQ, block % ZQ, lax.axis_index("zr"))]
    for ylo in range(YLO):
        found = lax.dot_general(
            rows_ref[...], weights_ref[ylo], (((1,), (1,)), ((), ())), preferred_element_type=f32
        ).astype(bf16)
        for place in range(3):
            for block in range(YLO * ZQ):
                t, low = block // 2, block % 2
                at, row = (low * 3 + place) * 16, (place * YLO * ZQ + block) * 16
                chunks_ref[Y_ORDER.index(t * YLO + ylo), at : at + 16] = found[row : row + 16]


def part_sums(parts_ref, average_ref, sent_ref):
    for ylo in range(YLO):
        total = sum(parts_ref[Y_ORDER.index(t * YLO + ylo)].astype(f32) for t in range(YHI)).astype(bf16)
        for x in range(X):
            sent_ref[x, ylo * 96 : (ylo + 1) * 96] = total
    for x in range(X):
        for k in range(9):
            at = YLO * 96 + k * ROWS
            sent_ref[X_ORDER.index(x), at : at + ROWS] = average_ref[x * ROWS : (x + 1) * ROWS, k * 128 : (k + 1) * 128]


def updates(joined_ref, params_ref, momentum_ref, half_ref, new_params_ref, new_momentum_ref):
    total = joined_ref[0, 0 : YLO * 96].astype(f32)
    for x in range(1, X):
        total = total + joined_ref[x, 0 : YLO * 96].astype(f32)
    half_ref[...] = total.astype(bf16)
    for x in range(X):
        for k in range(9):
            at, col = YLO * 96 + k * ROWS, x * COLS + k * 128
            average = joined_ref[X_ORDER.index(x), at : at + ROWS].astype(f32)
            moved = nesterov * momentum_ref[:, col : col + 128] + average
            new_momentum_ref[:, col : col + 128] = moved
            new_params_ref[:, col : col + 128] = params_ref[:, col : col + 128] - outer_rate * (
                average + nesterov * moved
            )


def placing(whole_ref, out_ref):
    zr = lax.axis_index("zr")
    for core in range(CORE):
        near_zr = neighbour_zr(core)
        for place in range(3):
            zr_of = zr if place == 2 else near_zr
            quarter = core if place == 2 else place
            for ylo in range(YLO):
                for low in range(2):
                    row = (low * ZR + zr_of) * 64 + (quarter * YLO + ylo) * 16
                    at = ylo * 96 + (low * 3 + place) * 16
                    out_ref[pl.ds(pl.multiple_of(row, 16), 16)] = whole_ref[core, at : at + 16]


def per_device(pseudo_grad, compensation, params, momentum, probe):
    x = lax.axis_index("x")

    grads, carried = (pltpu.with_memory_space_constraint(a, pltpu.HBM) for a in (pseudo_grad, compensation))
    copies, lent = pl.pallas_call(
        opening,
        out_shape=(jax.ShapeDtypeStruct((YLO * ZQ, 16, COLS), bf16), SUMS),
        in_specs=[ANY] * 3,
        out_specs=(ANY, VMEM),
        scratch_shapes=[
            pltpu.VMEM((YLO, 16, COLS), bf16),
            *SUMS_SCRATCH,
            pltpu.SemaphoreType.DMA((YLO + YLO * ZQ,)),
            pltpu.SemaphoreType.DMA((2, X)),
        ],
        name="opening",
        compiler_params=SMALL,
    )(pltpu.with_memory_space_constraint(probe, pltpu.HBM), grads, carried)
    far = exchange(copies, ("ylo", "zq", "zr"), FAR_ORDERS)
    lot = lax.all_gather(far, "core", axis=0)
    neighbours = [(z, z + 1) for z in range(0, Z, 2)] + [(Z + z, Z + (z + 1) % Z) for z in range(1, Z, 2)]
    near = swapped(lot, ("core", "zq", "zr"), neighbours)

    partners = swapped(lent, "core", [(0, 1)])
    kept = pl.pallas_call(
        own_rows,
        out_shape=SUMS,
        in_specs=[ANY] * 2,
        out_specs=VMEM,
        scratch_shapes=[*SUMS_SCRATCH, pltpu.SemaphoreType.DMA((2, X))],
        name="kept",
        compiler_params=SMALL,
    )(grads, carried)
    pair = (partners.astype(f32) + kept).astype(bf16)
    decayed = (params - (outer_rate * nesterov * nesterov) * momentum).astype(bf16)
    both = jnp.concatenate([pair, decayed], axis=0)

    def share(i):
        return lax.dynamic_slice_in_dim(both, lax.bitwise_xor(x, i) * COLS, COLS, axis=1)

    arrived = [share(0)]
    for i in range(1, X):
        arrived.append(swapped(share(i), "x", [(j, j ^ i) for j in range(X) if j < j ^ i]))
    average = sum(a[: X * ROWS].astype(f32) for a in arrived) / (X * CORE)
    places = jnp.stack([a[X * ROWS :] for a in arrived])
    base = jnp.concatenate([taken(places, lax.bitwise_xor(x, i)) for i in range(X)]).astype(f32)
    weights = (base - (outer_rate * (1 + nesterov)) * average).astype(bf16)

    two = lax.all_gather(weights, "ylo", axis=0)
    local_weights = lax.all_gather(two, "core", axis=0)
    chunks = pl.pallas_call(
        product,
        out_shape=jax.ShapeDtypeStruct((YHI * YLO, 96, 128), bf16),
        in_specs=[VMEM] * 3,
        out_specs=VMEM,
        scratch_shapes=[pltpu.VMEM((YLO, 128, COLS), bf16), pltpu.VMEM((3 * YLO * ZQ * 16, COLS), bf16)],
        name="product",
        compiler_params=SMALL,
    )(near, far, local_weights.reshape(CORE * YLO, X * ROWS, COLS))
    parts = exchange(chunks, ("yhi", "ylo"), [Y_ORDER])
    sent = pl.pallas_call(
        part_sums,
        out_shape=jax.ShapeDtypeStruct((X, YLO * 96 + 9 * ROWS, 128), bf16),
        in_specs=[VMEM] * 2,
        out_specs=VMEM,
        name="part_sums",
        compiler_params=SMALL,
    )(parts, average.astype(bf16))
    joined = exchange(sent, "x", [X_ORDER])
    half, new_params, new_momentum = pl.pallas_call(
        updates,
        out_shape=(
            jax.ShapeDtypeStruct((YLO * 96, 128), bf16),
            jax.ShapeDtypeStruct(params.shape, f32),
            jax.ShapeDtypeStruct(momentum.shape, f32),
        ),
        in_specs=[VMEM] * 3,
        out_specs=(VMEM,) * 3,
        name="updates",
        compiler_params=SMALL,
    )(joined, params, momentum)
    whole = lax.all_gather(half, "core", axis=0)
    probe_out = pl.pallas_call(
        placing,
        out_shape=jax.ShapeDtypeStruct((384, 128), bf16),
        in_specs=[VMEM],
        out_specs=VMEM,
        name="placing",
        compiler_params=SMALL,
    )(whole)
    return new_params, new_momentum, probe_out


def solution(mesh):
    fine = Mesh(
        mesh.devices.reshape(X, CORE, YLO, ZQ, ZR, YHI), ("x", "core", "ylo", "zq", "zr", "yhi")
    )
    whole, rows = ("x", "core"), ("ylo", "zq", "zr")
    shard = P((*rows, *whole), "yhi")
    in_specs = (P(whole, rows, "yhi"), P(whole, rows, "yhi"), shard, shard, P(rows, "yhi"))
    out_specs = (shard, shard, P("yhi", rows))

    return jax.shard_map(per_device, mesh=fine, in_specs=in_specs, out_specs=out_specs, check_vma=False)
```

time: 81.1 us -> 79.7 us (0.983)
  starting transfers between devices: 38.6 us -> 36 us
  blocking collectives: 33.4 us -> 35.9 us
  Pallas kernels: 7.05 us -> 6 us
    all_gather x0 -> x1, blocking collectives: none -> 3.08 us  [per_device(): lot = lax.all_gather(far, 'core', axis=0)]
    ppermute x6 -> x5, starting transfers between devices: 32.3 us -> 29.2 us  [swapped(): return lax.ppermute(x, axes, [*pairs, *((j, i) for i, j in pairs)])]
    all_gather x1, blocking collectives: 4.32 us -> 2.22 us  [per_device(): local_weights = lax.all_gather(two, 'core', axis=0)]
    pallas_call x3 -> x2, Pallas kernels: 4.78 us -> 3.74 us  [the longest x1 2.13 us: per_device(): pl.pallas_call(opening, out_shape=(jax.ShapeDtypeStruct((YLO * ZQ, 16, CO...]
    all_gather x1, blocking collectives: 4.95 us -> 5.96 us  [per_device(): two = lax.all_gather(weights, 'ylo', axis=0)]
  transfers between devices with their start and end apart: 7 -> 6, of which waited for: 1 -> 0; matrix products, arithmetic and copies ran while one was open for 1% -> 1% of each run, Pallas kernels for 4% -> 2%
where the time goes in v2:
time: 79.7 us; the launch traced here: 79.2 us
  starting transfers between devices  36 us (45%)
  blocking collectives  35.9 us (45%)
  Pallas kernels  6 us (8%)
  between operations  0.86 us (1%)
    ppermute x5, starting transfers between devices, swapped(): return lax.ppermute(x, axes, [*pairs, *((j, i) for i, j in pairs)])  29.2 us
    all_to_all x2, blocking collectives, exchange(): lax.all_to_all(tiles, axes, split_axis=0, concat_axis=0, tiled=True, axis...  21.1 us
    all_to_all x1, starting transfers between devices, exchange(): lax.all_to_all(tiles, axes, split_axis=0, concat_axis=0, tiled=True, axis...  6.73 us
    all_gather x1, blocking collectives, per_device(): two = lax.all_gather(weights, 'ylo', axis=0)  5.96 us
    all_gather x1, blocking collectives, per_device(): whole = lax.all_gather(half, 'core', axis=0)  3.56 us
    all_gather x1, blocking collectives, per_device(): lot = lax.all_gather(far, 'core', axis=0)  3.08 us
    all_gather x1, blocking collectives, per_device(): local_weights = lax.all_gather(two, 'core', axis=0)  2.22 us
    pallas_call x1, Pallas kernels, per_device(): pl.pallas_call(opening, out_shape=(jax.ShapeDtypeStruct((YLO * ZQ, 16, CO...  2.13 us
  transfers between devices with their start and end apart: 6, of which 0 were waited for; matrix products, arithmetic and copies ran while one was open for 1% of the time, Pallas kernels for 2%

profile of v2, /device:TPU:1, one launch (start us, length us, event | category | flops | bytes accessed | tf_op | source)
XLA Modules:
  0.0 79.2 jit_solution(12126047362942565766)
XLA Ops:
  0.6 2.1 %opening.1 = (bf16[8,16,1152]{2,1,0:T(8,128)(2,1)}, bf16[64,4608]{1,0:T(8,128)(2,1)S(1)}) custom-call(bf16[64,4608]{1,0:T(8,128)(2,1)} %probe_ref.1, bf16[1,128,4608]{2,1,0:T(8,128)(2,1)} %grads_ref.3, f32[1,128,4608]{2,1,0:T(8,128)} %carried_ref.3), custom_call_target="tpu_custom_call" | custom-call | tf_op jit(solution)/shard_map/opening/pallas_call | solution.py:182
  2.8 12.4 %collective-permute-start.1 = (bf16[64,4608]{1,0:T(8,128)(2,1)S(1)}, bf16[64,4608]{1,0:T(8,128)(2,1)S(1)}, u32[]{:S(2)}, u32[]{:S(2)}) collective-permute-start(bf16[64,4608]{1,0:T(8,128)(2,1)S(1)} %get-tuple-element.9), channel_id=1, source_target_pairs={{0,96},{96,0},{1,97},{97,1},{2,98},{98,2},{3,99},{99,3},{4,100},{1... | collective-permute-start | bytes 1769480 | tf_op jit(solution)/shard_map/ppermute | solution.py:38
  15.1 6.7 %all-to-all-start = ((bf16[8,16,1152]{2,1,0:T(8,128)(2,1)}), bf16[8,16,1152]{2,1,0:T(8,128)(2,1)S(1)}, u32[]{:S(2)}, u32[]{:S(2)}) async-start(bf16[8,16,1152]{2,1,0:T(8,128)(2,1)} %get-tuple-element.8), calls=%async_computation | async-start | bytes 589824 | tf_op jit(solution)/shard_map/all_to_all | solution.py:23
  21.9 0.0 copy-start
  21.9 0.0 copy-start.1
  21.9 1.6 %kept.1 = bf16[64,4608]{1,0:T(8,128)(2,1)S(1)} custom-call(bf16[1,128,4608]{2,1,0:T(8,128)(2,1)} %grads_ref.3, f32[1,128,4608]{2,1,0:T(8,128)} %carried_ref.3), custom_call_target="tpu_custom_call" | custom-call | tf_op jit(solution)/shard_map/kept/pallas_call | solution.py:202
  23.5 0.0 copy-done
  23.5 0.0 copy-done.1
  23.6 0.0 collective-permute-done.1
  23.6 0.1 add_convert_fusion
  23.8 0.1 fusion.1
  23.8 4.4 %collective-permute-start.4 = (bf16[80,1152]{1,0:T(8,128)(2,1)S(1)}, bf16[80,1152]{1,0:T(8,128)(2,1)S(1)}, u32[]{:S(2)}, u32[]{:S(2)}) collective-permute-start(bf16[80,1152]{1,0:T(8,128)(2,1)S(1)} %get-tuple-element.18), channel_id=1, source_target_pairs={{0,576},{192,384},{576,0},{384,192},{1,577},{193,385},{577,1},{385... | collective-permute-start | bytes 552968 | tf_op jit(solution)/shard_map/ppermute | solution.py:38
  28.2 2.4 %collective-permute-start.3 = (bf16[80,1152]{1,0:T(8,128)(2,1)S(1)}, bf16[80,1152]{1,0:T(8,128)(2,1)S(1)}, u32[]{:S(2)}, u32[]{:S(2)}) collective-permute-start(bf16[80,1152]{1,0:T(8,128)(2,1)S(1)} %get-tuple-element.17), channel_id=1, source_target_pairs={{0,384},{192,576},{384,0},{576,192},{1,385},{193,577},{385,1},{577... | collective-permute-start | bytes 552968 | tf_op jit(solution)/shard_map/ppermute | solution.py:38
  30.7 2.2 %collective-permute-start.2 = (bf16[80,1152]{1,0:T(8,128)(2,1)S(1)}, bf16[80,1152]{1,0:T(8,128)(2,1)S(1)}, u32[]{:S(2)}, u32[]{:S(2)}) collective-permute-start(bf16[80,1152]{1,0:T(8,128)(2,1)S(1)} %get-tuple-element.16), channel_id=1, source_target_pairs={{0,192},{384,576},{192,0},{576,384},{1,193},{385,577},{193,1},{577... | collective-permute-start | bytes 552968 | tf_op jit(solution)/shard_map/ppermute | solution.py:38
  32.8 0.0 all-to-all-done.far_ref
  32.9 3.1 %all-gather = bf16[16,16,1152]{2,1,0:T(8,128)(2,1)S(1)} all-gather(bf16[8,16,1152]{2,1,0:T(8,128)(2,1)S(1)} %all-to-all-done.far_ref), channel_id=2, replica_groups=mesh['x'=4,'core'=2,'ylo'=2,'zq'=4,'zr'=3,'yhi'=4] {'core'}, dimensions={0}, use_global_device_ids=true | all-gather | bytes 884736 | tf_op jit(solution)/shard_map/all_gather | solution.py:197
  35.9 7.9 %collective-permute-start = (bf16[2,8,16,1152]{3,2,1,0:T(8,128)(2,1)S(1)}, bf16[2,8,16,1152]{3,2,1,0:T(8,128)(2,1)S(1)}, u32[]{:S(2)}, u32[]{:S(2)}) collective-permute-start(bf16[2,8,16,1152]{3,2,1,0:T(8,128)(2,1)S(1)} %bitcast.21), channel_id=1, source_target_pairs={{0,4},{8,12},{16,20},{24,28},{32,36},{40,44},{100,104},{108,112},{... | collective-permute-start | bytes 1769480 | tf_op jit(solution)/shard_map/ppermute | solution.py:38
  43.9 0.0 collective-permute-done.4
  43.9 0.0 collective-permute-done.3
  43.9 0.0 collective-permute-done.2
  44.0 0.1 multiply_convert_fusion
  44.1 6.0 %all-gather.1 = bf16[128,1152]{1,0:T(8,128)(2,1)S(1)} all-gather(bf16[64,1152]{1,0:T(8,128)(2,1)S(1)} %get-tuple-element.14), channel_id=3, replica_groups=mesh['x'=4,'core'=2,'ylo'=2,'zq'=4,'zr'=3,'yhi'=4] {'ylo'}, dimensions={0}, use_global_device_ids=true | all-gather | bytes 442368 | tf_op jit(solution)/shard_map/all_gather | solution.py:226
  50.1 2.2 %all-gather.2.gathered_ref = bf16[4,64,1152]{2,1,0:T(8,128)(2,1)S(1)} all-gather(bf16[2,64,1152]{2,1,0:T(8,128)(2,1)S(1)} %bitcast.20), channel_id=4, replica_groups=mesh['x'=4,'core'=2,'ylo'=2,'zq'=4,'zr'=3,'yhi'=4] {'core'}, dimensions={0}, use_global_device_ids=true | all-gather | bytes 884736 | tf_op jit(solution)/shard_map/all_gather | solution.py:227
  52.3 0.0 collective-permute-done.near_ref
  52.3 0.7 product.1
  53.0 12.4 %all_to_all.15.parts_ref = bf16[8,96,128]{2,1,0:T(8,128)(2,1)S(1)} all-to-all(bf16[8,96,128]{2,1,0:T(8,128)(2,1)S(1)} %product.1), channel_id=1, replica_groups={{2,49,1,48,0,51,3,50},{6,53,5,52,4,55,7,54},{10,57,9,56,8,59,11,58},{14..., dimensions={0} | all-to-all | bytes 393216 | tf_op jit(solution)/shard_map/all_to_all | solution.py:23
  65.5 8.6 %all_to_all.16.joined_ref = bf16[4,336,128]{2,1,0:T(8,128)(2,1)S(1)} all-to-all(bf16[4,336,128]{2,1,0:T(8,128)(2,1)S(1)} %part_sums.1), channel_id=1, replica_groups={{384,0,192,576},{385,1,193,577},{386,2,194,578},{387,3,195,579},{388,4,..., dimensions={0} | all-to-all | bytes 688128 | tf_op jit(solution)/shard_map/all_to_all | solution.py:23
  74.1 0.9 %updates.1 = (bf16[192,128]{1,0:T(8,128)(2,1)S(1)}, f32[16,4608]{1,0:T(8,128)}, f32[16,4608]{1,0:T(8,128)}) custom-call(bf16[4,336,128]{2,1,0:T(8,128)(2,1)S(1)} %all_to_all.16.joined_ref, f32[16,4608]{1,0:T(8,128)S(1)} %copy-done, f32[16,4608]{1,0:T(8,128)S(1)} %copy-done.1), custom_call_target="tpu_custom_call" | custom-call | tf_op jit(solution)/shard_map/updates/pallas_call | solution.py:247
  75.0 3.6 %all-gather.3 = bf16[384,128]{1,0:T(8,128)(2,1)S(1)} all-gather(bf16[192,128]{1,0:T(8,128)(2,1)S(1)} %get-tuple-element.12), channel_id=5, replica_groups=mesh['x'=4,'core'=2,'ylo'=2,'zq'=4,'zr'=3,'yhi'=4] {'core'}, dimensions={0}, use_global_device_ids=true | all-gather | bytes 147456 | tf_op jit(solution)/shard_map/all_gather | solution.py:259
  78.5 0.7 placing.1
  (8 shorter events, 0.1 us)
Async XLA Ops:
  2.8 20.8 %collective-permute-start.1 = (bf16[64,4608]{1,0:T(8,128)(2,1)S(1)}, bf16[64,4608]{1,0:T(8,128)(2,1)S(1)}, u32[]{:S(2)}, u32[]{:S(2)}) collective-permute-start(bf16[64,4608]{1,0:T(8,128)(2,1)S(1)} %get-tuple-element.9), channel_id=1, source_target_pairs={{0,96},{96,0},{1,97},{97,1},{2,98},{98,2},{3,99},{99,3},{4,100},{1... | collective-permute-start | bytes 1769480 | tf_op jit(solution)/shard_map/ppermute | solution.py:38
  15.1 17.7 %all-to-all-start = ((bf16[8,16,1152]{2,1,0:T(8,128)(2,1)}), bf16[8,16,1152]{2,1,0:T(8,128)(2,1)S(1)}, u32[]{:S(2)}, u32[]{:S(2)}) async-start(bf16[8,16,1152]{2,1,0:T(8,128)(2,1)} %get-tuple-element.8), calls=%async_computation | async-start | bytes 589824 | tf_op jit(solution)/shard_map/all_to_all | solution.py:23
  21.9 1.7 %copy-start = (f32[16,4608]{1,0:T(8,128)S(1)}, f32[16,4608]{1,0:T(8,128)}, u32[]{:S(2)}) copy-start(f32[16,4608]{1,0:T(8,128)} %params_ref.1) | copy-start | bytes 884740
  21.9 1.7 %copy-start.1 = (f32[16,4608]{1,0:T(8,128)S(1)}, f32[16,4608]{1,0:T(8,128)}, u32[]{:S(2)}) copy-start(f32[16,4608]{1,0:T(8,128)} %momentum_ref.1) | copy-start | bytes 884740
  23.8 20.0 %collective-permute-start.4 = (bf16[80,1152]{1,0:T(8,128)(2,1)S(1)}, bf16[80,1152]{1,0:T(8,128)(2,1)S(1)}, u32[]{:S(2)}, u32[]{:S(2)}) collective-permute-start(bf16[80,1152]{1,0:T(8,128)(2,1)S(1)} %get-tuple-element.18), channel_id=1, source_target_pairs={{0,576},{192,384},{576,0},{384,192},{1,577},{193,385},{577,1},{385... | collective-permute-start | bytes 552968 | tf_op jit(solution)/shard_map/ppermute | solution.py:38
  28.2 15.7 %collective-permute-start.3 = (bf16[80,1152]{1,0:T(8,128)(2,1)S(1)}, bf16[80,1152]{1,0:T(8,128)(2,1)S(1)}, u32[]{:S(2)}, u32[]{:S(2)}) collective-permute-start(bf16[80,1152]{1,0:T(8,128)(2,1)S(1)} %get-tuple-element.17), channel_id=1, source_target_pairs={{0,384},{192,576},{384,0},{576,192},{1,385},{193,577},{385,1},{577... | collective-permute-start | bytes 552968 | tf_op jit(solution)/shard_map/ppermute | solution.py:38
  30.7 13.2 %collective-permute-start.2 = (bf16[80,1152]{1,0:T(8,128)(2,1)S(1)}, bf16[80,1152]{1,0:T(8,128)(2,1)S(1)}, u32[]{:S(2)}, u32[]{:S(2)}) collective-permute-start(bf16[80,1152]{1,0:T(8,128)(2,1)S(1)} %get-tuple-element.16), channel_id=1, source_target_pairs={{0,192},{384,576},{192,0},{576,384},{1,193},{385,577},{193,1},{577... | collective-permute-start | bytes 552968 | tf_op jit(solution)/shard_map/ppermute | solution.py:38
  35.9 16.4 %collective-permute-start = (bf16[2,8,16,1152]{3,2,1,0:T(8,128)(2,1)S(1)}, bf16[2,8,16,1152]{3,2,1,0:T(8,128)(2,1)S(1)}, u32[]{:S(2)}, u32[]{:S(2)}) collective-permute-start(bf16[2,8,16,1152]{3,2,1,0:T(8,128)(2,1)S(1)} %bitcast.21), channel_id=1, source_target_pairs={{0,4},{8,12},{16,20},{24,28},{32,36},{40,44},{100,104},{108,112},{... | collective-permute-start | bytes 1769480 | tf_op jit(solution)/shard_map/ppermute | solution.py:38

commit v3 on v2

--- a/solution.py
+++ b/solution.py
@@ -145,23 +145,11 @@
             sent_ref[X_ORDER.index(x), at : at + ROWS] = average_ref[x * ROWS : (x + 1) * ROWS, k * 128 : (k + 1) * 128]
 
 
-def updates(joined_ref, params_ref, momentum_ref, half_ref, new_params_ref, new_momentum_ref):
-    total = joined_ref[0, 0 : YLO * 96].astype(f32)
-    for x in range(1, X):
-        total = total + joined_ref[x, 0 : YLO * 96].astype(f32)
-    half_ref[...] = total.astype(bf16)
-    for x in range(X):
-        for k in range(9):
-            at, col = YLO * 96 + k * ROWS, x * COLS + k * 128
-            average = joined_ref[X_ORDER.index(x), at : at + ROWS].astype(f32)
-            moved = nesterov * momentum_ref[:, col : col + 128] + average
-            new_momentum_ref[:, col : col + 128] = moved
-            new_params_ref[:, col : col + 128] = params_ref[:, col : col + 128] - outer_rate * (
-                average + nesterov * moved
-            )
-
-
-def placing(whole_ref, out_ref):
+def halves(joined_ref, half_ref):
+    half_ref[...] = sum(joined_ref[x, 0 : YLO * 96].astype(f32) for x in range(X)).astype(bf16)
+
+
+def closing(whole_ref, joined_ref, params_ref, momentum_ref, new_params_ref, new_momentum_ref, out_ref):
     zr = lax.axis_index("zr")
     for core in range(CORE):
         near_zr = neighbour_zr(core)
@@ -173,6 +161,15 @@
                     row = (low * ZR + zr_of) * 64 + (quarter * YLO + ylo) * 16
                     at = ylo * 96 + (low * 3 + place) * 16
                     out_ref[pl.ds(pl.multiple_of(row, 16), 16)] = whole_ref[core, at : at + 16]
+    for x in range(X):
+        for k in range(9):
+            at, col = YLO * 96 + k * ROWS, x * COLS + k * 128
+            average = joined_ref[X_ORDER.index(x), at : at + ROWS].astype(f32)
+            moved = nesterov * momentum_ref[:, col : col + 128] + average
+            new_momentum_ref[:, col : col + 128] = moved
+            new_params_ref[:, col : col + 128] = params_ref[:, col : col + 128] - outer_rate * (
+                average + nesterov * moved
+            )
 
 
 def per_device(pseudo_grad, compensation, params, momentum, probe):
@@ -244,28 +241,27 @@
         compiler_params=SMALL,
     )(parts, average.astype(bf16))
     joined = exchange(sent, "x", [X_ORDER])
-    half, new_params, new_momentum = pl.pallas_call(
-        updates,
+    half = pl.pallas_call(
+        halves,
+        out_shape=jax.ShapeDtypeStruct((YLO * 96, 128), bf16),
+        in_specs=[VMEM],
+        out_specs=VMEM,
+        name="halves",
+        compiler_params=SMALL,
+    )(joined)
+    whole = lax.all_gather(half, "core", axis=0)
+    return pl.pallas_call(
+        closing,
         out_shape=(
-            jax.ShapeDtypeStruct((YLO * 96, 128), bf16),
             jax.ShapeDtypeStruct(params.shape, f32),
             jax.ShapeDtypeStruct(momentum.shape, f32),
+            jax.ShapeDtypeStruct((384, 128), bf16),
         ),
-        in_specs=[VMEM] * 3,
+        in_specs=[VMEM] * 4,
         out_specs=(VMEM,) * 3,
-        name="updates",
-        compiler_params=SMALL,
-    )(joined, params, momentum)
-    whole = lax.all_gather(half, "core", axis=0)
-    probe_out = pl.pallas_call(
-        placing,
-        out_shape=jax.ShapeDtypeStruct((384, 128), bf16),
-        in_specs=[VMEM],
-        out_specs=VMEM,
-        name="placing",
-        compiler_params=SMALL,
-    )(whole)
-    return new_params, new_momentum, probe_out
+        name="closing",
+        compiler_params=SMALL,
+    )(whole, joined, params, momentum)
 
 
 def solution(mesh):

time: 79.7 us -> 79.2 us (level)
  no operation moved by 1% of the time
where the time goes in v3:
time: 79.2 us; the launch traced here: 78.7 us
  starting transfers between devices  36 us (45%)
  blocking collectives  35.9 us (45%)
  Pallas kernels  5.43 us (7%)
  between operations  0.87 us (1%)
    ppermute x5, starting transfers between devices, swapped(): return lax.ppermute(x, axes, [*pairs, *((j, i) for i, j in pairs)])  29.2 us
    all_to_all x2, blocking collectives, exchange(): lax.all_to_all(tiles, axes, split_axis=0, concat_axis=0, tiled=True, axis...  21.1 us
    all_to_all x1, starting transfers between devices, exchange(): lax.all_to_all(tiles, axes, split_axis=0, concat_axis=0, tiled=True, axis...  6.73 us
    all_gather x1, blocking collectives, per_device(): two = lax.all_gather(weights, 'ylo', axis=0)  5.96 us
    all_gather x1, blocking collectives, per_device(): whole = lax.all_gather(half, 'core', axis=0)  3.57 us
    all_gather x1, blocking collectives, per_device(): lot = lax.all_gather(far, 'core', axis=0)  3.08 us
    all_gather x1, blocking collectives, per_device(): local_weights = lax.all_gather(two, 'core', axis=0)  2.22 us
    pallas_call x1, Pallas kernels, per_device(): pl.pallas_call(opening, out_shape=(jax.ShapeDtypeStruct((YLO * ZQ, 16, CO...  2.13 us
  transfers between devices with their start and end apart: 6, of which 0 were waited for; matrix products, arithmetic and copies ran while one was open for 1% of the time, Pallas kernels for 2%

profile of v3, /device:TPU:1, one launch (start us, length us, event | category | flops | bytes accessed | tf_op | source)
XLA Modules:
  0.0 78.7 jit_solution(10589377770953301118)
XLA Ops:
  0.6 2.1 %opening.1 = (bf16[8,16,1152]{2,1,0:T(8,128)(2,1)}, bf16[64,4608]{1,0:T(8,128)(2,1)S(1)}) custom-call(bf16[64,4608]{1,0:T(8,128)(2,1)} %probe_ref.1, bf16[1,128,4608]{2,1,0:T(8,128)(2,1)} %grads_ref.3, f32[1,128,4608]{2,1,0:T(8,128)} %carried_ref.3), custom_call_target="tpu_custom_call" | custom-call | tf_op jit(solution)/shard_map/opening/pallas_call | solution.py:179
  2.8 12.4 %collective-permute-start.1 = (bf16[64,4608]{1,0:T(8,128)(2,1)S(1)}, bf16[64,4608]{1,0:T(8,128)(2,1)S(1)}, u32[]{:S(2)}, u32[]{:S(2)}) collective-permute-start(bf16[64,4608]{1,0:T(8,128)(2,1)S(1)} %get-tuple-element.6), channel_id=1, source_target_pairs={{0,96},{96,0},{1,97},{97,1},{2,98},{98,2},{3,99},{99,3},{4,100},{1... | collective-permute-start | bytes 1769480 | tf_op jit(solution)/shard_map/ppermute | solution.py:38
  15.1 6.7 %all-to-all-start = ((bf16[8,16,1152]{2,1,0:T(8,128)(2,1)}), bf16[8,16,1152]{2,1,0:T(8,128)(2,1)S(1)}, u32[]{:S(2)}, u32[]{:S(2)}) async-start(bf16[8,16,1152]{2,1,0:T(8,128)(2,1)} %get-tuple-element.5), calls=%async_computation | async-start | bytes 589824 | tf_op jit(solution)/shard_map/all_to_all | solution.py:23
  21.9 0.0 copy-start
  21.9 0.0 copy-start.1
  21.9 1.6 %kept.1 = bf16[64,4608]{1,0:T(8,128)(2,1)S(1)} custom-call(bf16[1,128,4608]{2,1,0:T(8,128)(2,1)} %grads_ref.3, f32[1,128,4608]{2,1,0:T(8,128)} %carried_ref.3), custom_call_target="tpu_custom_call" | custom-call | tf_op jit(solution)/shard_map/kept/pallas_call | solution.py:199
  23.5 0.0 copy-done
  23.5 0.0 copy-done.1
  23.6 0.0 collective-permute-done.1
  23.6 0.1 add_convert_fusion
  23.8 0.1 fusion.1
  23.8 4.4 %collective-permute-start.4 = (bf16[80,1152]{1,0:T(8,128)(2,1)S(1)}, bf16[80,1152]{1,0:T(8,128)(2,1)S(1)}, u32[]{:S(2)}, u32[]{:S(2)}) collective-permute-start(bf16[80,1152]{1,0:T(8,128)(2,1)S(1)} %get-tuple-element.12), channel_id=1, source_target_pairs={{0,576},{192,384},{576,0},{384,192},{1,577},{193,385},{577,1},{385... | collective-permute-start | bytes 552968 | tf_op jit(solution)/shard_map/ppermute | solution.py:38
  28.2 2.4 %collective-permute-start.3 = (bf16[80,1152]{1,0:T(8,128)(2,1)S(1)}, bf16[80,1152]{1,0:T(8,128)(2,1)S(1)}, u32[]{:S(2)}, u32[]{:S(2)}) collective-permute-start(bf16[80,1152]{1,0:T(8,128)(2,1)S(1)} %get-tuple-element.11), channel_id=1, source_target_pairs={{0,384},{192,576},{384,0},{576,192},{1,385},{193,577},{385,1},{577... | collective-permute-start | bytes 552968 | tf_op jit(solution)/shard_map/ppermute | solution.py:38
  30.7 2.2 %collective-permute-start.2 = (bf16[80,1152]{1,0:T(8,128)(2,1)S(1)}, bf16[80,1152]{1,0:T(8,128)(2,1)S(1)}, u32[]{:S(2)}, u32[]{:S(2)}) collective-permute-start(bf16[80,1152]{1,0:T(8,128)(2,1)S(1)} %get-tuple-element.10), channel_id=1, source_target_pairs={{0,192},{384,576},{192,0},{576,384},{1,193},{385,577},{193,1},{577... | collective-permute-start | bytes 552968 | tf_op jit(solution)/shard_map/ppermute | solution.py:38
  32.8 0.0 all-to-all-done.far_ref
  32.9 3.1 %all-gather = bf16[16,16,1152]{2,1,0:T(8,128)(2,1)S(1)} all-gather(bf16[8,16,1152]{2,1,0:T(8,128)(2,1)S(1)} %all-to-all-done.far_ref), channel_id=2, replica_groups=mesh['x'=4,'core'=2,'ylo'=2,'zq'=4,'zr'=3,'yhi'=4] {'core'}, dimensions={0}, use_global_device_ids=true | all-gather | bytes 884736 | tf_op jit(solution)/shard_map/all_gather | solution.py:194
  35.9 7.9 %collective-permute-start = (bf16[2,8,16,1152]{3,2,1,0:T(8,128)(2,1)S(1)}, bf16[2,8,16,1152]{3,2,1,0:T(8,128)(2,1)S(1)}, u32[]{:S(2)}, u32[]{:S(2)}) collective-permute-start(bf16[2,8,16,1152]{3,2,1,0:T(8,128)(2,1)S(1)} %bitcast.21), channel_id=1, source_target_pairs={{0,4},{8,12},{16,20},{24,28},{32,36},{40,44},{100,104},{108,112},{... | collective-permute-start | bytes 1769480 | tf_op jit(solution)/shard_map/ppermute | solution.py:38
  43.9 0.0 collective-permute-done.4
  43.9 0.0 collective-permute-done.3
  43.9 0.0 collective-permute-done.2
  44.0 0.1 multiply_convert_fusion
  44.1 6.0 %all-gather.1 = bf16[128,1152]{1,0:T(8,128)(2,1)S(1)} all-gather(bf16[64,1152]{1,0:T(8,128)(2,1)S(1)} %get-tuple-element.8), channel_id=3, replica_groups=mesh['x'=4,'core'=2,'ylo'=2,'zq'=4,'zr'=3,'yhi'=4] {'ylo'}, dimensions={0}, use_global_device_ids=true | all-gather | bytes 442368 | tf_op jit(solution)/shard_map/all_gather | solution.py:223
  50.1 2.2 %all-gather.2.gathered_ref = bf16[4,64,1152]{2,1,0:T(8,128)(2,1)S(1)} all-gather(bf16[2,64,1152]{2,1,0:T(8,128)(2,1)S(1)} %bitcast.20), channel_id=4, replica_groups=mesh['x'=4,'core'=2,'ylo'=2,'zq'=4,'zr'=3,'yhi'=4] {'core'}, dimensions={0}, use_global_device_ids=true | all-gather | bytes 884736 | tf_op jit(solution)/shard_map/all_gather | solution.py:224
  52.3 0.0 collective-permute-done.near_ref
  52.3 0.7 product.1
  53.0 12.4 %all_to_all.15.parts_ref = bf16[8,96,128]{2,1,0:T(8,128)(2,1)S(1)} all-to-all(bf16[8,96,128]{2,1,0:T(8,128)(2,1)S(1)} %product.1), channel_id=1, replica_groups={{2,49,1,48,0,51,3,50},{6,53,5,52,4,55,7,54},{10,57,9,56,8,59,11,58},{14..., dimensions={0} | all-to-all | bytes 393216 | tf_op jit(solution)/shard_map/all_to_all | solution.py:23
  65.5 8.6 %all_to_all.16.joined_ref = bf16[4,336,128]{2,1,0:T(8,128)(2,1)S(1)} all-to-all(bf16[4,336,128]{2,1,0:T(8,128)(2,1)S(1)} %part_sums.1), channel_id=1, replica_groups={{384,0,192,576},{385,1,193,577},{386,2,194,578},{387,3,195,579},{388,4,..., dimensions={0} | all-to-all | bytes 688128 | tf_op jit(solution)/shard_map/all_to_all | solution.py:23
  74.1 3.6 %all-gather.3 = bf16[384,128]{1,0:T(8,128)(2,1)S(1)} all-gather(bf16[192,128]{1,0:T(8,128)(2,1)S(1)} %halves.1), channel_id=5, replica_groups=mesh['x'=4,'core'=2,'ylo'=2,'zq'=4,'zr'=3,'yhi'=4] {'core'}, dimensions={0}, use_global_device_ids=true | all-gather | bytes 147456 | tf_op jit(solution)/shard_map/all_gather | solution.py:252
  77.7 0.9 %closing.1 = (f32[16,4608]{1,0:T(8,128)}, f32[16,4608]{1,0:T(8,128)}, bf16[384,128]{1,0:T(8,128)(2,1)}) custom-call(bf16[2,192,128]{2,1,0:T(8,128)(2,1)S(1)} %bitcast.19, bf16[4,336,128]{2,1,0:T(8,128)(2,1)S(1)} %all_to_all.16.joined_ref, f32[16,4608]{1,0:T(8,128)S(1)} %copy-done, f32[16,4608]{1,0:T(8,128)S(1)} %copy-done.1), custom_call_target="tpu_custom_call" | custom-call | tf_op jit(solution)/shard_map/closing/pallas_call | solution.py:253
  (9 shorter events, 0.2 us)
Async XLA Ops:
  2.8 20.8 %collective-permute-start.1 = (bf16[64,4608]{1,0:T(8,128)(2,1)S(1)}, bf16[64,4608]{1,0:T(8,128)(2,1)S(1)}, u32[]{:S(2)}, u32[]{:S(2)}) collective-permute-start(bf16[64,4608]{1,0:T(8,128)(2,1)S(1)} %get-tuple-element.6), channel_id=1, source_target_pairs={{0,96},{96,0},{1,97},{97,1},{2,98},{98,2},{3,99},{99,3},{4,100},{1... | collective-permute-start | bytes 1769480 | tf_op jit(solution)/shard_map/ppermute | solution.py:38
  15.1 17.7 %all-to-all-start = ((bf16[8,16,1152]{2,1,0:T(8,128)(2,1)}), bf16[8,16,1152]{2,1,0:T(8,128)(2,1)S(1)}, u32[]{:S(2)}, u32[]{:S(2)}) async-start(bf16[8,16,1152]{2,1,0:T(8,128)(2,1)} %get-tuple-element.5), calls=%async_computation | async-start | bytes 589824 | tf_op jit(solution)/shard_map/all_to_all | solution.py:23
  21.9 1.7 %copy-start = (f32[16,4608]{1,0:T(8,128)S(1)}, f32[16,4608]{1,0:T(8,128)}, u32[]{:S(2)}) copy-start(f32[16,4608]{1,0:T(8,128)} %params_ref.1) | copy-start | bytes 884740
  21.9 1.7 %copy-start.1 = (f32[16,4608]{1,0:T(8,128)S(1)}, f32[16,4608]{1,0:T(8,128)}, u32[]{:S(2)}) copy-start(f32[16,4608]{1,0:T(8,128)} %momentum_ref.1) | copy-start | bytes 884740
  23.8 20.0 %collective-permute-start.4 = (bf16[80,1152]{1,0:T(8,128)(2,1)S(1)}, bf16[80,1152]{1,0:T(8,128)(2,1)S(1)}, u32[]{:S(2)}, u32[]{:S(2)}) collective-permute-start(bf16[80,1152]{1,0:T(8,128)(2,1)S(1)} %get-tuple-element.12), channel_id=1, source_target_pairs={{0,576},{192,384},{576,0},{384,192},{1,577},{193,385},{577,1},{385... | collective-permute-start | bytes 552968 | tf_op jit(solution)/shard_map/ppermute | solution.py:38
  28.2 15.7 %collective-permute-start.3 = (bf16[80,1152]{1,0:T(8,128)(2,1)S(1)}, bf16[80,1152]{1,0:T(8,128)(2,1)S(1)}, u32[]{:S(2)}, u32[]{:S(2)}) collective-permute-start(bf16[80,1152]{1,0:T(8,128)(2,1)S(1)} %get-tuple-element.11), channel_id=1, source_target_pairs={{0,384},{192,576},{384,0},{576,192},{1,385},{193,577},{385,1},{577... | collective-permute-start | bytes 552968 | tf_op jit(solution)/shard_map/ppermute | solution.py:38
  30.7 13.2 %collective-permute-start.2 = (bf16[80,1152]{1,0:T(8,128)(2,1)S(1)}, bf16[80,1152]{1,0:T(8,128)(2,1)S(1)}, u32[]{:S(2)}, u32[]{:S(2)}) collective-permute-start(bf16[80,1152]{1,0:T(8,128)(2,1)S(1)} %get-tuple-element.10), channel_id=1, source_target_pairs={{0,192},{384,576},{192,0},{576,384},{1,193},{385,577},{193,1},{577... | collective-permute-start | bytes 552968 | tf_op jit(solution)/shard_map/ppermute | solution.py:38
  35.9 16.4 %collective-permute-start = (bf16[2,8,16,1152]{3,2,1,0:T(8,128)(2,1)S(1)}, bf16[2,8,16,1152]{3,2,1,0:T(8,128)(2,1)S(1)}, u32[]{:S(2)}, u32[]{:S(2)}) collective-permute-start(bf16[2,8,16,1152]{3,2,1,0:T(8,128)(2,1)S(1)} %bitcast.21), channel_id=1, source_target_pairs={{0,4},{8,12},{16,20},{24,28},{32,36},{40,44},{100,104},{108,112},{... | collective-permute-start | bytes 1769480 | tf_op jit(solution)/shard_map/ppermute | solution.py:38

commit v4 on v3

--- a/solution.py
+++ b/solution.py
@@ -14,7 +14,7 @@
 X, CORE, YLO, ZQ, ZR, YHI = 4, 2, 2, 4, 3, 4
 Z = ZQ * ZR
 Y_ORDER = [4, 3, 2, 1, 0, 7, 6, 5]
-X_ORDER = [2, 0, 1, 3]
+X_ORDER = [2, 0, 3, 1]
 ROWS = 16
 COLS = 1152
 
@@ -23,15 +23,18 @@
     return lax.all_to_all(tiles, axes, split_axis=0, concat_axis=0, tiled=True, axis_index_groups=orders)
 
 
-LEADS = (3, 3, 2)
+LEADS = (3, 0, 0)
 FAR_ORDERS = [
     [(ylo * ZQ + (lead + n) % ZQ) * ZR + zr for ylo in range(YLO) for n in range(ZQ)] for zr, lead in enumerate(LEADS)
 ]
 
 
+def lead_of(zr):
+    return jnp.where(zr == 0, LEADS[0], jnp.where(zr == 1, LEADS[1], LEADS[2]))
+
+
 def far_place(ylo, zq, zr):
-    lead = jnp.where(zr == 0, LEADS[0], jnp.where(zr == 1, LEADS[1], LEADS[2]))
-    return ylo * ZQ + lax.rem(zq + ZQ - lead, ZQ)
+    return ylo * ZQ + lax.rem(zq + ZQ - lead_of(zr), ZQ)
 
 
 def swapped(x, axes, pairs):
@@ -109,29 +112,29 @@
     return lax.rem(zr + 1 + odd, ZR)
 
 
-def product(near_ref, far_ref, gathered_ref, chunks_ref, weights_ref, rows_ref):
+def product(near_ref, far_ref, gathered_ref, chunks_ref, weights_ref):
     for ylo in range(YLO):
         for x in range(X):
             for core in range(CORE):
-                at = (x * CORE + core) * ROWS
-                weights_ref[ylo, at : at + ROWS] = gathered_ref[core * YLO + ylo, x * ROWS : (x + 1) * ROWS]
-    near_zr = neighbour_zr(lax.axis_index("core"))
+                at = ylo * 128 + (x * CORE + core) * ROWS
+                weights_ref[at : at + ROWS] = gathered_ref[core * YLO + ylo, x * ROWS : (x + 1) * ROWS]
+    near_lead = lead_of(neighbour_zr(lax.axis_index("core")))
+    own_lead = lead_of(lax.axis_index("zr"))
     for place in range(3):
-        for block in range(YLO * ZQ):
-            row = (place * YLO * ZQ + block) * 16
-            if place < 2:
-                rows_ref[row : row + 16] = near_ref[place, far_place(block // ZQ, block % ZQ, near_zr)]
-            else:
-                rows_ref[row : row + 16] = far_ref[far_place(block // ZQ, block % ZQ, lax.axis_index("zr"))]
-    for ylo in range(YLO):
+        ref, lead = (near_ref.at[place], near_lead) if place < 2 else (far_ref, own_lead)
         found = lax.dot_general(
-            rows_ref[...], weights_ref[ylo], (((1,), (1,)), ((), ())), preferred_element_type=f32
+            ref[...].reshape(YLO * ZQ * 16, COLS), weights_ref[...], (((1,), (1,)), ((), ())), preferred_element_type=f32
         ).astype(bf16)
-        for place in range(3):
-            for block in range(YLO * ZQ):
-                t, low = block // 2, block % 2
-                at, row = (low * 3 + place) * 16, (place * YLO * ZQ + block) * 16
-                chunks_ref[Y_ORDER.index(t * YLO + ylo), at : at + 16] = found[row : row + 16]
+        for n in range(ZQ):
+            zq = lax.rem(n + lead, ZQ)
+            at = pl.multiple_of((lax.rem(zq, 2) * 3 + place) * 16, 16)
+            for ylo in range(YLO):
+                row = (ylo * ZQ + n) * 16
+                for side in range(YLO):
+                    low, high = (Y_ORDER.index((ylo * 2 + half) * YLO + side) for half in range(2))
+                    chunks_ref[jnp.where(zq < 2, low, high), pl.ds(at, 16)] = found[
+                        row : row + 16, side * 128 : (side + 1) * 128
+                    ]
 
 
 def part_sums(parts_ref, average_ref, sent_ref):
@@ -227,7 +230,7 @@
         out_shape=jax.ShapeDtypeStruct((YHI * YLO, 96, 128), bf16),
         in_specs=[VMEM] * 3,
         out_specs=VMEM,
-        scratch_shapes=[pltpu.VMEM((YLO, 128, COLS), bf16), pltpu.VMEM((3 * YLO * ZQ * 16, COLS), bf16)],
+        scratch_shapes=[pltpu.VMEM((YLO * 128, COLS), bf16)],
         name="product",
         compiler_params=SMALL,
     )(near, far, local_weights.reshape(CORE * YLO, X * ROWS, COLS))

time: 79.2 us -> 78.2 us (0.987)
  starting transfers between devices: 36 us -> 34.1 us
  blocking collectives: 35.9 us -> 36.9 us
    ppermute x5, starting transfers between devices: 29.2 us -> 27.3 us  [swapped(): return lax.ppermute(x, axes, [*pairs, *((j, i) for i, j in pairs)])]
    all_gather x1, blocking collectives: 2.22 us -> 3.74 us  [per_device(): local_weights = lax.all_gather(two, 'core', axis=0)]
    all_gather x1, blocking collectives: 5.96 us -> 5.03 us  [per_device(): two = lax.all_gather(weights, 'ylo', axis=0)]
where the time goes in v4:
time: 78.2 us; the launch traced here: 77.7 us
  blocking collectives  36.9 us (47%)
  starting transfers between devices  34.1 us (44%)
  Pallas kernels  5.39 us (7%)
  between operations  0.87 us (1%)
    ppermute x5, starting transfers between devices, swapped(): return lax.ppermute(x, axes, [*pairs, *((j, i) for i, j in pairs)])  27.3 us
    all_to_all x2, blocking collectives, exchange(): lax.all_to_all(tiles, axes, split_axis=0, concat_axis=0, tiled=True, axis...  21.5 us
    all_to_all x1, starting transfers between devices, exchange(): lax.all_to_all(tiles, axes, split_axis=0, concat_axis=0, tiled=True, axis...  6.73 us
    all_gather x1, blocking collectives, per_device(): two = lax.all_gather(weights, 'ylo', axis=0)  5.03 us
    all_gather x1, blocking collectives, per_device(): local_weights = lax.all_gather(two, 'core', axis=0)  3.74 us
    all_gather x1, blocking collectives, per_device(): whole = lax.all_gather(half, 'core', axis=0)  3.56 us
    all_gather x1, blocking collectives, per_device(): lot = lax.all_gather(far, 'core', axis=0)  3.08 us
    pallas_call x1, Pallas kernels, per_device(): pl.pallas_call(opening, out_shape=(jax.ShapeDtypeStruct((YLO * ZQ, 16, CO...  2.13 us
  transfers between devices with their start and end apart: 6, of which 0 were waited for; matrix products, arithmetic and copies ran while one was open for 1% of the time, Pallas kernels for 2%

profile of v4, /device:TPU:1, one launch (start us, length us, event | category | flops | bytes accessed | tf_op | source)
XLA Modules:
  0.0 77.7 jit_solution(6939840018780586422)
XLA Ops:
  0.6 2.1 %opening.1 = (bf16[8,16,1152]{2,1,0:T(8,128)(2,1)}, bf16[64,4608]{1,0:T(8,128)(2,1)S(1)}) custom-call(bf16[64,4608]{1,0:T(8,128)(2,1)} %probe_ref.1, bf16[1,128,4608]{2,1,0:T(8,128)(2,1)} %grads_ref.3, f32[1,128,4608]{2,1,0:T(8,128)} %carried_ref.3), custom_call_target="tpu_custom_call" | custom-call | tf_op jit(solution)/shard_map/opening/pallas_call | solution.py:182
  2.8 12.4 %collective-permute-start.1 = (bf16[64,4608]{1,0:T(8,128)(2,1)S(1)}, bf16[64,4608]{1,0:T(8,128)(2,1)S(1)}, u32[]{:S(2)}, u32[]{:S(2)}) collective-permute-start(bf16[64,4608]{1,0:T(8,128)(2,1)S(1)} %get-tuple-element.6), channel_id=1, source_target_pairs={{0,96},{96,0},{1,97},{97,1},{2,98},{98,2},{3,99},{99,3},{4,100},{1... | collective-permute-start | bytes 1769480 | tf_op jit(solution)/shard_map/ppermute | solution.py:41
  15.1 6.7 %all-to-all-start = ((bf16[8,16,1152]{2,1,0:T(8,128)(2,1)}), bf16[8,16,1152]{2,1,0:T(8,128)(2,1)S(1)}, u32[]{:S(2)}, u32[]{:S(2)}) async-start(bf16[8,16,1152]{2,1,0:T(8,128)(2,1)} %get-tuple-element.5), calls=%async_computation | async-start | bytes 589824 | tf_op jit(solution)/shard_map/all_to_all | solution.py:23
  21.9 0.0 copy-start
  21.9 0.0 copy-start.1
  21.9 1.6 %kept.1 = bf16[64,4608]{1,0:T(8,128)(2,1)S(1)} custom-call(bf16[1,128,4608]{2,1,0:T(8,128)(2,1)} %grads_ref.3, f32[1,128,4608]{2,1,0:T(8,128)} %carried_ref.3), custom_call_target="tpu_custom_call" | custom-call | tf_op jit(solution)/shard_map/kept/pallas_call | solution.py:202
  23.5 0.0 copy-done
  23.5 0.0 copy-done.1
  23.6 0.0 collective-permute-done.1
  23.6 0.1 add_convert_fusion
  23.8 0.1 fusion.1
  23.8 4.4 %collective-permute-start.4 = (bf16[80,1152]{1,0:T(8,128)(2,1)S(1)}, bf16[80,1152]{1,0:T(8,128)(2,1)S(1)}, u32[]{:S(2)}, u32[]{:S(2)}) collective-permute-start(bf16[80,1152]{1,0:T(8,128)(2,1)S(1)} %get-tuple-element.12), channel_id=1, source_target_pairs={{0,576},{192,384},{576,0},{384,192},{1,577},{193,385},{577,1},{385... | collective-permute-start | bytes 552968 | tf_op jit(solution)/shard_map/ppermute | solution.py:41
  28.2 2.4 %collective-permute-start.3 = (bf16[80,1152]{1,0:T(8,128)(2,1)S(1)}, bf16[80,1152]{1,0:T(8,128)(2,1)S(1)}, u32[]{:S(2)}, u32[]{:S(2)}) collective-permute-start(bf16[80,1152]{1,0:T(8,128)(2,1)S(1)} %get-tuple-element.11), channel_id=1, source_target_pairs={{0,384},{192,576},{384,0},{576,192},{1,385},{193,577},{385,1},{577... | collective-permute-start | bytes 552968 | tf_op jit(solution)/shard_map/ppermute | solution.py:41
  30.7 2.2 %collective-permute-start.2 = (bf16[80,1152]{1,0:T(8,128)(2,1)S(1)}, bf16[80,1152]{1,0:T(8,128)(2,1)S(1)}, u32[]{:S(2)}, u32[]{:S(2)}) collective-permute-start(bf16[80,1152]{1,0:T(8,128)(2,1)S(1)} %get-tuple-element.10), channel_id=1, source_target_pairs={{0,192},{384,576},{192,0},{576,384},{1,193},{385,577},{193,1},{577... | collective-permute-start | bytes 552968 | tf_op jit(solution)/shard_map/ppermute | solution.py:41
  32.8 0.0 all-to-all-done.far_ref
  32.9 3.1 %all-gather = bf16[16,16,1152]{2,1,0:T(8,128)(2,1)S(1)} all-gather(bf16[8,16,1152]{2,1,0:T(8,128)(2,1)S(1)} %all-to-all-done.far_ref), channel_id=2, replica_groups=mesh['x'=4,'core'=2,'ylo'=2,'zq'=4,'zr'=3,'yhi'=4] {'core'}, dimensions={0}, use_global_device_ids=true | all-gather | bytes 884736 | tf_op jit(solution)/shard_map/all_gather | solution.py:197
  35.9 6.0 %collective-permute-start = (bf16[2,8,16,1152]{3,2,1,0:T(8,128)(2,1)S(1)}, bf16[2,8,16,1152]{3,2,1,0:T(8,128)(2,1)S(1)}, u32[]{:S(2)}, u32[]{:S(2)}) collective-permute-start(bf16[2,8,16,1152]{3,2,1,0:T(8,128)(2,1)S(1)} %bitcast.21), channel_id=1, source_target_pairs={{0,4},{8,12},{16,20},{24,28},{32,36},{40,44},{100,104},{108,112},{... | collective-permute-start | bytes 1769480 | tf_op jit(solution)/shard_map/ppermute | solution.py:41
  42.0 0.0 collective-permute-done.4
  42.0 0.0 collective-permute-done.3
  42.0 0.0 collective-permute-done.2
  42.1 0.1 multiply_convert_fusion
  42.2 5.0 %all-gather.1 = bf16[128,1152]{1,0:T(8,128)(2,1)S(1)} all-gather(bf16[64,1152]{1,0:T(8,128)(2,1)S(1)} %get-tuple-element.8), channel_id=3, replica_groups=mesh['x'=4,'core'=2,'ylo'=2,'zq'=4,'zr'=3,'yhi'=4] {'ylo'}, dimensions={0}, use_global_device_ids=true | all-gather | bytes 442368 | tf_op jit(solution)/shard_map/all_gather | solution.py:226
  47.3 3.7 %all-gather.2.gathered_ref = bf16[4,64,1152]{2,1,0:T(8,128)(2,1)S(1)} all-gather(bf16[2,64,1152]{2,1,0:T(8,128)(2,1)S(1)} %bitcast.20), channel_id=4, replica_groups=mesh['x'=4,'core'=2,'ylo'=2,'zq'=4,'zr'=3,'yhi'=4] {'core'}, dimensions={0}, use_global_device_ids=true | all-gather | bytes 884736 | tf_op jit(solution)/shard_map/all_gather | solution.py:227
  51.0 0.0 collective-permute-done.near_ref
  51.0 0.6 product.1
  51.7 12.9 %all_to_all.15.parts_ref = bf16[8,96,128]{2,1,0:T(8,128)(2,1)S(1)} all-to-all(bf16[8,96,128]{2,1,0:T(8,128)(2,1)S(1)} %product.1), channel_id=1, replica_groups={{2,49,1,48,0,51,3,50},{6,53,5,52,4,55,7,54},{10,57,9,56,8,59,11,58},{14..., dimensions={0} | all-to-all | bytes 393216 | tf_op jit(solution)/shard_map/all_to_all | solution.py:23
  64.6 8.6 %all_to_all.16.joined_ref = bf16[4,336,128]{2,1,0:T(8,128)(2,1)S(1)} all-to-all(bf16[4,336,128]{2,1,0:T(8,128)(2,1)S(1)} %part_sums.1), channel_id=1, replica_groups={{384,0,576,192},{385,1,577,193},{386,2,578,194},{387,3,579,195},{388,4,..., dimensions={0} | all-to-all | bytes 688128 | tf_op jit(solution)/shard_map/all_to_all | solution.py:23
  73.2 3.6 %all-gather.3 = bf16[384,128]{1,0:T(8,128)(2,1)S(1)} all-gather(bf16[192,128]{1,0:T(8,128)(2,1)S(1)} %halves.1), channel_id=5, replica_groups=mesh['x'=4,'core'=2,'ylo'=2,'zq'=4,'zr'=3,'yhi'=4] {'core'}, dimensions={0}, use_global_device_ids=true | all-gather | bytes 147456 | tf_op jit(solution)/shard_map/all_gather | solution.py:255
  76.8 0.9 %closing.1 = (f32[16,4608]{1,0:T(8,128)}, f32[16,4608]{1,0:T(8,128)}, bf16[384,128]{1,0:T(8,128)(2,1)}) custom-call(bf16[2,192,128]{2,1,0:T(8,128)(2,1)S(1)} %bitcast.19, bf16[4,336,128]{2,1,0:T(8,128)(2,1)S(1)} %all_to_all.16.joined_ref, f32[16,4608]{1,0:T(8,128)S(1)} %copy-done, f32[16,4608]{1,0:T(8,128)S(1)} %copy-done.1), custom_call_target="tpu_custom_call" | custom-call | tf_op jit(solution)/shard_map/closing/pallas_call | solution.py:256
  (9 shorter events, 0.2 us)
Async XLA Ops:
  2.8 20.8 %collective-permute-start.1 = (bf16[64,4608]{1,0:T(8,128)(2,1)S(1)}, bf16[64,4608]{1,0:T(8,128)(2,1)S(1)}, u32[]{:S(2)}, u32[]{:S(2)}) collective-permute-start(bf16[64,4608]{1,0:T(8,128)(2,1)S(1)} %get-tuple-element.6), channel_id=1, source_target_pairs={{0,96},{96,0},{1,97},{97,1},{2,98},{98,2},{3,99},{99,3},{4,100},{1... | collective-permute-start | bytes 1769480 | tf_op jit(solution)/shard_map/ppermute | solution.py:41
  15.1 17.7 %all-to-all-start = ((bf16[8,16,1152]{2,1,0:T(8,128)(2,1)}), bf16[8,16,1152]{2,1,0:T(8,128)(2,1)S(1)}, u32[]{:S(2)}, u32[]{:S(2)}) async-start(bf16[8,16,1152]{2,1,0:T(8,128)(2,1)} %get-tuple-element.5), calls=%async_computation | async-start | bytes 589824 | tf_op jit(solution)/shard_map/all_to_all | solution.py:23
  21.9 1.7 %copy-start = (f32[16,4608]{1,0:T(8,128)S(1)}, f32[16,4608]{1,0:T(8,128)}, u32[]{:S(2)}) copy-start(f32[16,4608]{1,0:T(8,128)} %params_ref.1) | copy-start | bytes 884740
  21.9 1.7 %copy-start.1 = (f32[16,4608]{1,0:T(8,128)S(1)}, f32[16,4608]{1,0:T(8,128)}, u32[]{:S(2)}) copy-start(f32[16,4608]{1,0:T(8,128)} %momentum_ref.1) | copy-start | bytes 884740
  23.8 18.1 %collective-permute-start.4 = (bf16[80,1152]{1,0:T(8,128)(2,1)S(1)}, bf16[80,1152]{1,0:T(8,128)(2,1)S(1)}, u32[]{:S(2)}, u32[]{:S(2)}) collective-permute-start(bf16[80,1152]{1,0:T(8,128)(2,1)S(1)} %get-tuple-element.12), channel_id=1, source_target_pairs={{0,576},{192,384},{576,0},{384,192},{1,577},{193,385},{577,1},{385... | collective-permute-start | bytes 552968 | tf_op jit(solution)/shard_map/ppermute | solution.py:41
  28.2 13.8 %collective-permute-start.3 = (bf16[80,1152]{1,0:T(8,128)(2,1)S(1)}, bf16[80,1152]{1,0:T(8,128)(2,1)S(1)}, u32[]{:S(2)}, u32[]{:S(2)}) collective-permute-start(bf16[80,1152]{1,0:T(8,128)(2,1)S(1)} %get-tuple-element.11), channel_id=1, source_target_pairs={{0,384},{192,576},{384,0},{576,192},{1,385},{193,577},{385,1},{577... | collective-permute-start | bytes 552968 | tf_op jit(solution)/shard_map/ppermute | solution.py:41
  30.7 11.3 %collective-permute-start.2 = (bf16[80,1152]{1,0:T(8,128)(2,1)S(1)}, bf16[80,1152]{1,0:T(8,128)(2,1)S(1)}, u32[]{:S(2)}, u32[]{:S(2)}) collective-permute-start(bf16[80,1152]{1,0:T(8,128)(2,1)S(1)} %get-tuple-element.10), channel_id=1, source_target_pairs={{0,192},{384,576},{192,0},{576,384},{1,193},{385,577},{193,1},{577... | collective-permute-start | bytes 552968 | tf_op jit(solution)/shard_map/ppermute | solution.py:41
  35.9 15.1 %collective-permute-start = (bf16[2,8,16,1152]{3,2,1,0:T(8,128)(2,1)S(1)}, bf16[2,8,16,1152]{3,2,1,0:T(8,128)(2,1)S(1)}, u32[]{:S(2)}, u32[]{:S(2)}) collective-permute-start(bf16[2,8,16,1152]{3,2,1,0:T(8,128)(2,1)S(1)} %bitcast.21), channel_id=1, source_target_pairs={{0,4},{8,12},{16,20},{24,28},{32,36},{40,44},{100,104},{108,112},{... | collective-permute-start | bytes 1769480 | tf_op jit(solution)/shard_map/ppermute | solution.py:41

commit v5 on v4

--- a/solution.py
+++ b/solution.py
@@ -60,9 +60,10 @@
             pltpu.make_async_copy(grads_ref.at[0, pl.ds(row, ROWS)], grad_ref.at[x], sems.at[0, x]),
             pltpu.make_async_copy(carried_ref.at[0, pl.ds(row, ROWS)], carry_ref.at[x], sems.at[1, x]),
         )
-        for copy in pair:
-            copy.start()
         copies.append(pair)
+    for n in (1, 0):
+        for pair in copies:
+            pair[n].start()
     return copies
 
 

time: 78.2 us -> 78.3 us (level)
  no operation moved by 1% of the time
where the time goes in v5:
time: 78.3 us; the launch traced here: 77.8 us
  blocking collectives  36.9 us (47%)
  starting transfers between devices  34.2 us (44%)
  Pallas kernels  5.31 us (7%)
  between operations  0.87 us (1%)
    ppermute x5, starting transfers between devices, swapped(): return lax.ppermute(x, axes, [*pairs, *((j, i) for i, j in pairs)])  27.5 us
    all_to_all x2, blocking collectives, exchange(): lax.all_to_all(tiles, axes, split_axis=0, concat_axis=0, tiled=True, axis...  21.5 us
    all_to_all x1, starting transfers between devices, exchange(): lax.all_to_all(tiles, axes, split_axis=0, concat_axis=0, tiled=True, axis...  6.73 us
    all_gather x1, blocking collectives, per_device(): two = lax.all_gather(weights, 'ylo', axis=0)  5.03 us
    all_gather x1, blocking collectives, per_device(): local_weights = lax.all_gather(two, 'core', axis=0)  3.74 us
    all_gather x1, blocking collectives, per_device(): whole = lax.all_gather(half, 'core', axis=0)  3.56 us
    all_gather x1, blocking collectives, per_device(): lot = lax.all_gather(far, 'core', axis=0)  3.08 us
    pallas_call x1, Pallas kernels, per_device(): pl.pallas_call(opening, out_shape=(jax.ShapeDtypeStruct((YLO * ZQ, 16, CO...  2.11 us
  transfers between devices with their start and end apart: 6, of which 0 were waited for; matrix products, arithmetic and copies ran while one was open for 1% of the time, Pallas kernels for 2%

profile of v5, /device:TPU:1, one launch (start us, length us, event | category | flops | bytes accessed | tf_op | source)
XLA Modules:
  0.0 77.8 jit_solution(9455279811931460332)
XLA Ops:
  0.6 2.1 %opening.1 = (bf16[8,16,1152]{2,1,0:T(8,128)(2,1)}, bf16[64,4608]{1,0:T(8,128)(2,1)S(1)}) custom-call(bf16[64,4608]{1,0:T(8,128)(2,1)} %probe_ref.1, bf16[1,128,4608]{2,1,0:T(8,128)(2,1)} %grads_ref.3, f32[1,128,4608]{2,1,0:T(8,128)} %carried_ref.3), custom_call_target="tpu_custom_call" | custom-call | tf_op jit(solution)/shard_map/opening/pallas_call | solution.py:183
  2.7 12.4 %collective-permute-start.1 = (bf16[64,4608]{1,0:T(8,128)(2,1)S(1)}, bf16[64,4608]{1,0:T(8,128)(2,1)S(1)}, u32[]{:S(2)}, u32[]{:S(2)}) collective-permute-start(bf16[64,4608]{1,0:T(8,128)(2,1)S(1)} %get-tuple-element.6), channel_id=1, source_target_pairs={{0,96},{96,0},{1,97},{97,1},{2,98},{98,2},{3,99},{99,3},{4,100},{1... | collective-permute-start | bytes 1769480 | tf_op jit(solution)/shard_map/ppermute | solution.py:41
  15.2 6.7 %all-to-all-start = ((bf16[8,16,1152]{2,1,0:T(8,128)(2,1)}), bf16[8,16,1152]{2,1,0:T(8,128)(2,1)S(1)}, u32[]{:S(2)}, u32[]{:S(2)}) async-start(bf16[8,16,1152]{2,1,0:T(8,128)(2,1)} %get-tuple-element.5), calls=%async_computation | async-start | bytes 589824 | tf_op jit(solution)/shard_map/all_to_all | solution.py:23
  21.9 0.0 copy-start
  21.9 0.0 copy-start.1
  21.9 1.6 %kept.1 = bf16[64,4608]{1,0:T(8,128)(2,1)S(1)} custom-call(bf16[1,128,4608]{2,1,0:T(8,128)(2,1)} %grads_ref.3, f32[1,128,4608]{2,1,0:T(8,128)} %carried_ref.3), custom_call_target="tpu_custom_call" | custom-call | tf_op jit(solution)/shard_map/kept/pallas_call | solution.py:203
  23.5 0.0 copy-done
  23.5 0.0 copy-done.1
  23.6 0.0 collective-permute-done.1
  23.6 0.1 add_convert_fusion
  23.8 0.1 fusion.1
  23.8 4.4 %collective-permute-start.4 = (bf16[80,1152]{1,0:T(8,128)(2,1)S(1)}, bf16[80,1152]{1,0:T(8,128)(2,1)S(1)}, u32[]{:S(2)}, u32[]{:S(2)}) collective-permute-start(bf16[80,1152]{1,0:T(8,128)(2,1)S(1)} %get-tuple-element.12), channel_id=1, source_target_pairs={{0,576},{192,384},{576,0},{384,192},{1,577},{193,385},{577,1},{385... | collective-permute-start | bytes 552968 | tf_op jit(solution)/shard_map/ppermute | solution.py:41
  28.2 2.5 %collective-permute-start.3 = (bf16[80,1152]{1,0:T(8,128)(2,1)S(1)}, bf16[80,1152]{1,0:T(8,128)(2,1)S(1)}, u32[]{:S(2)}, u32[]{:S(2)}) collective-permute-start(bf16[80,1152]{1,0:T(8,128)(2,1)S(1)} %get-tuple-element.11), channel_id=1, source_target_pairs={{0,384},{192,576},{384,0},{576,192},{1,385},{193,577},{385,1},{577... | collective-permute-start | bytes 552968 | tf_op jit(solution)/shard_map/ppermute | solution.py:41
  30.7 2.2 %collective-permute-start.2 = (bf16[80,1152]{1,0:T(8,128)(2,1)S(1)}, bf16[80,1152]{1,0:T(8,128)(2,1)S(1)}, u32[]{:S(2)}, u32[]{:S(2)}) collective-permute-start(bf16[80,1152]{1,0:T(8,128)(2,1)S(1)} %get-tuple-element.10), channel_id=1, source_target_pairs={{0,192},{384,576},{192,0},{576,384},{1,193},{385,577},{193,1},{577... | collective-permute-start | bytes 552968 | tf_op jit(solution)/shard_map/ppermute | solution.py:41
  32.9 0.0 all-to-all-done.far_ref
  32.9 3.1 %all-gather = bf16[16,16,1152]{2,1,0:T(8,128)(2,1)S(1)} all-gather(bf16[8,16,1152]{2,1,0:T(8,128)(2,1)S(1)} %all-to-all-done.far_ref), channel_id=2, replica_groups=mesh['x'=4,'core'=2,'ylo'=2,'zq'=4,'zr'=3,'yhi'=4] {'core'}, dimensions={0}, use_global_device_ids=true | all-gather | bytes 884736 | tf_op jit(solution)/shard_map/all_gather | solution.py:198
  35.9 6.1 %collective-permute-start = (bf16[2,8,16,1152]{3,2,1,0:T(8,128)(2,1)S(1)}, bf16[2,8,16,1152]{3,2,1,0:T(8,128)(2,1)S(1)}, u32[]{:S(2)}, u32[]{:S(2)}) collective-permute-start(bf16[2,8,16,1152]{3,2,1,0:T(8,128)(2,1)S(1)} %bitcast.21), channel_id=1, source_target_pairs={{0,4},{8,12},{16,20},{24,28},{32,36},{40,44},{100,104},{108,112},{... | collective-permute-start | bytes 1769480 | tf_op jit(solution)/shard_map/ppermute | solution.py:41
  42.0 0.0 collective-permute-done.4
  42.0 0.0 collective-permute-done.3
  42.1 0.0 collective-permute-done.2
  42.2 0.1 multiply_convert_fusion
  42.3 5.0 %all-gather.1 = bf16[128,1152]{1,0:T(8,128)(2,1)S(1)} all-gather(bf16[64,1152]{1,0:T(8,128)(2,1)S(1)} %get-tuple-element.8), channel_id=3, replica_groups=mesh['x'=4,'core'=2,'ylo'=2,'zq'=4,'zr'=3,'yhi'=4] {'ylo'}, dimensions={0}, use_global_device_ids=true | all-gather | bytes 442368 | tf_op jit(solution)/shard_map/all_gather | solution.py:227
  47.3 3.7 %all-gather.2.gathered_ref = bf16[4,64,1152]{2,1,0:T(8,128)(2,1)S(1)} all-gather(bf16[2,64,1152]{2,1,0:T(8,128)(2,1)S(1)} %bitcast.20), channel_id=4, replica_groups=mesh['x'=4,'core'=2,'ylo'=2,'zq'=4,'zr'=3,'yhi'=4] {'core'}, dimensions={0}, use_global_device_ids=true | all-gather | bytes 884736 | tf_op jit(solution)/shard_map/all_gather | solution.py:228
  51.1 0.0 collective-permute-done.near_ref
  51.1 0.6 product.1
  51.7 12.9 %all_to_all.15.parts_ref = bf16[8,96,128]{2,1,0:T(8,128)(2,1)S(1)} all-to-all(bf16[8,96,128]{2,1,0:T(8,128)(2,1)S(1)} %product.1), channel_id=1, replica_groups={{2,49,1,48,0,51,3,50},{6,53,5,52,4,55,7,54},{10,57,9,56,8,59,11,58},{14..., dimensions={0} | all-to-all | bytes 393216 | tf_op jit(solution)/shard_map/all_to_all | solution.py:23
  64.6 8.6 %all_to_all.16.joined_ref = bf16[4,336,128]{2,1,0:T(8,128)(2,1)S(1)} all-to-all(bf16[4,336,128]{2,1,0:T(8,128)(2,1)S(1)} %part_sums.1), channel_id=1, replica_groups={{384,0,576,192},{385,1,577,193},{386,2,578,194},{387,3,579,195},{388,4,..., dimensions={0} | all-to-all | bytes 688128 | tf_op jit(solution)/shard_map/all_to_all | solution.py:23
  73.3 3.6 %all-gather.3 = bf16[384,128]{1,0:T(8,128)(2,1)S(1)} all-gather(bf16[192,128]{1,0:T(8,128)(2,1)S(1)} %halves.1), channel_id=5, replica_groups=mesh['x'=4,'core'=2,'ylo'=2,'zq'=4,'zr'=3,'yhi'=4] {'core'}, dimensions={0}, use_global_device_ids=true | all-gather | bytes 147456 | tf_op jit(solution)/shard_map/all_gather | solution.py:256
  76.8 0.9 %closing.1 = (f32[16,4608]{1,0:T(8,128)}, f32[16,4608]{1,0:T(8,128)}, bf16[384,128]{1,0:T(8,128)(2,1)}) custom-call(bf16[2,192,128]{2,1,0:T(8,128)(2,1)S(1)} %bitcast.19, bf16[4,336,128]{2,1,0:T(8,128)(2,1)S(1)} %all_to_all.16.joined_ref, f32[16,4608]{1,0:T(8,128)S(1)} %copy-done, f32[16,4608]{1,0:T(8,128)S(1)} %copy-done.1), custom_call_target="tpu_custom_call" | custom-call | tf_op jit(solution)/shard_map/closing/pallas_call | solution.py:257
  (9 shorter events, 0.2 us)
Async XLA Ops:
  2.7 20.9 %collective-permute-start.1 = (bf16[64,4608]{1,0:T(8,128)(2,1)S(1)}, bf16[64,4608]{1,0:T(8,128)(2,1)S(1)}, u32[]{:S(2)}, u32[]{:S(2)}) collective-permute-start(bf16[64,4608]{1,0:T(8,128)(2,1)S(1)} %get-tuple-element.6), channel_id=1, source_target_pairs={{0,96},{96,0},{1,97},{97,1},{2,98},{98,2},{3,99},{99,3},{4,100},{1... | collective-permute-start | bytes 1769480 | tf_op jit(solution)/shard_map/ppermute | solution.py:41
  15.2 17.7 %all-to-all-start = ((bf16[8,16,1152]{2,1,0:T(8,128)(2,1)}), bf16[8,16,1152]{2,1,0:T(8,128)(2,1)S(1)}, u32[]{:S(2)}, u32[]{:S(2)}) async-start(bf16[8,16,1152]{2,1,0:T(8,128)(2,1)} %get-tuple-element.5), calls=%async_computation | async-start | bytes 589824 | tf_op jit(solution)/shard_map/all_to_all | solution.py:23
  21.9 1.6 %copy-start = (f32[16,4608]{1,0:T(8,128)S(1)}, f32[16,4608]{1,0:T(8,128)}, u32[]{:S(2)}) copy-start(f32[16,4608]{1,0:T(8,128)} %params_ref.1) | copy-start | bytes 884740
  21.9 1.6 %copy-start.1 = (f32[16,4608]{1,0:T(8,128)S(1)}, f32[16,4608]{1,0:T(8,128)}, u32[]{:S(2)}) copy-start(f32[16,4608]{1,0:T(8,128)} %momentum_ref.1) | copy-start | bytes 884740
  23.8 18.2 %collective-permute-start.4 = (bf16[80,1152]{1,0:T(8,128)(2,1)S(1)}, bf16[80,1152]{1,0:T(8,128)(2,1)S(1)}, u32[]{:S(2)}, u32[]{:S(2)}) collective-permute-start(bf16[80,1152]{1,0:T(8,128)(2,1)S(1)} %get-tuple-element.12), channel_id=1, source_target_pairs={{0,576},{192,384},{576,0},{384,192},{1,577},{193,385},{577,1},{385... | collective-permute-start | bytes 552968 | tf_op jit(solution)/shard_map/ppermute | solution.py:41
  28.2 13.8 %collective-permute-start.3 = (bf16[80,1152]{1,0:T(8,128)(2,1)S(1)}, bf16[80,1152]{1,0:T(8,128)(2,1)S(1)}, u32[]{:S(2)}, u32[]{:S(2)}) collective-permute-start(bf16[80,1152]{1,0:T(8,128)(2,1)S(1)} %get-tuple-element.11), channel_id=1, source_target_pairs={{0,384},{192,576},{384,0},{576,192},{1,385},{193,577},{385,1},{577... | collective-permute-start | bytes 552968 | tf_op jit(solution)/shard_map/ppermute | solution.py:41
  30.7 11.4 %collective-permute-start.2 = (bf16[80,1152]{1,0:T(8,128)(2,1)S(1)}, bf16[80,1152]{1,0:T(8,128)(2,1)S(1)}, u32[]{:S(2)}, u32[]{:S(2)}) collective-permute-start(bf16[80,1152]{1,0:T(8,128)(2,1)S(1)} %get-tuple-element.10), channel_id=1, source_target_pairs={{0,192},{384,576},{192,0},{576,384},{1,193},{385,577},{193,1},{577... | collective-permute-start | bytes 552968 | tf_op jit(solution)/shard_map/ppermute | solution.py:41
  35.9 15.1 %collective-permute-start = (bf16[2,8,16,1152]{3,2,1,0:T(8,128)(2,1)S(1)}, bf16[2,8,16,1152]{3,2,1,0:T(8,128)(2,1)S(1)}, u32[]{:S(2)}, u32[]{:S(2)}) collective-permute-start(bf16[2,8,16,1152]{3,2,1,0:T(8,128)(2,1)S(1)} %bitcast.21), channel_id=1, source_target_pairs={{0,4},{8,12},{16,20},{24,28},{32,36},{40,44},{100,104},{108,112},{... | collective-permute-start | bytes 1769480 | tf_op jit(solution)/shard_map/ppermute | solution.py:41
